TPU v7x, 32 devices: a whole 2x2x4 slice. The times are simulated.
32 devices in a mesh: grp: 4 (over x, core), blk: 2 (over y), set: 4 (over z).
Axes of the slice: x: 2, y: 2, z: 4, core: 2. Of those that a mesh axis runs over, the one named last changes fastest.
Arguments:
- queries: bfloat16 [4096, 384], P(('grp', 'blk', 'set')), may hold values from -8 to 8
- keys: bfloat16 [4096, 384], P(('grp', 'blk', 'set')), may hold values from -8 to 8
- values: bfloat16 [4096, 384], P(('grp', 'blk', 'set')), may hold values from -6 to 6
- valid: int32 [4096], P(('grp', 'blk', 'set')), may hold values 0 or 1
- offsets: int32 [2, 6], replicated, may hold values from 0 to 7, as said below
- w_out: bfloat16 [384, 768], replicated, may hold values from -0.3125 to 0.3125
Outputs:
- projected: bfloat16 [4096, 768], P(('grp', 'blk', 'set'))
Inputs may be any that keep to these rules, and one draw needn't show every extreme that they name: offsets[0, h] lies in 0 to 1 and offsets[1, h] - offsets[0, h] is a multiple of 2 for every head h.
All inputs are finite; a program needn't handle non-finite values. No bound on the sum of `valid` on one device may be relied on, other than what follows from the above.
Results may differ from a plain program's by a relative error of at most 0.0015.
The roundings to bfloat16 on the way count: a program that leaves them out, or rounds other values in their place, can miss the bound.
Values may be sent and summed in bfloat16 or wider, within the bound.
A program may use at most 64 MiB of HBM per device.

v0:
```python
import functools

import jax
import jax.numpy as jnp
from jax import lax
from jax.experimental import pallas as pl
from jax.experimental.pallas import tpu as pltpu
from jax.sharding import PartitionSpec as P

HEAD_COUNT = 6
HD = 64
LANES = 128
UNIT = 16
FLAG_STRIDE = 8
CHUNKS = HEAD_COUNT * HD // LANES
MESH = pl.DeviceIdType.MESH
NEG = -1e30


def units(count):
    return -(-count // UNIT)


def split_pow2(x, size):
    shift = size.bit_length() - 1
    return lax.shift_right_logical(x, shift), x & (size - 1)


class Plan:
    def __init__(self, grp, blk, n, rows):
        self.grp, self.blk, self.n, self.rows = grp, blk, n, rows
        self.period = grp * blk
        self.c3 = rows // self.period
        c2 = rows // blk
        self.counts = (self.c3, c2 - self.c3, rows - c2)
        self.units = tuple(units(c) for c in self.counts)
        self.sizes = tuple(u * UNIT for u in self.units)
        self.starts = (0, self.sizes[0], self.sizes[0] + self.sizes[1])
        self.total = sum(self.sizes)

    def source(self, t):
        a = t
        b = t - self.starts[1]
        c = t - self.starts[2]
        bv, bg = split_pow2(b, self.c3)
        cv, cg = split_pow2(c, self.c3)
        ck, cm = split_pow2(cv, self.grp)
        is_a = t < self.starts[1]
        is_b = t < self.starts[2]
        group = jnp.where(is_a, a, jnp.where(is_b, bg, cg))
        slot = jnp.where(is_a, 0, jnp.where(is_b, (bv + 1) * self.blk, cm * self.blk + ck + 1))
        local = jnp.where(is_a, a, jnp.where(is_b, b, c))
        count = jnp.where(is_a, self.counts[0], jnp.where(is_b, self.counts[1], self.counts[2]))
        return jnp.where(local < count, group * self.period, -(1 << 20)), slot


def kernel(
    plan, q_ref, k_ref, v_ref, valid_ref, offs_ref, w_ref, o_ref,
    buf_a, buf_b, buf_c, qs, zrecv, zsend, yrecv, ysend, xrecv, xsend, fsend,
):
    G, B, N = plan.grp, plan.blk, plan.n
    R = plan.total
    gi, bi, si = lax.axis_index("grp"), lax.axis_index("blk"), lax.axis_index("set")
    core = gi % 2
    partner = gi + 1 - 2 * core

    def peer_grp(step):
        return lax.rem(gi + 2 * step, G)

    barrier = pltpu.get_barrier_semaphore()

    def greet(g, b, s):
        pl.semaphore_signal(barrier, inc=1, device_id=(g, b, s), device_id_type=MESH)

    @pl.when(si > 0)
    def _():
        greet(gi, bi, si - 1)

    @pl.when(si < N - 1)
    def _():
        greet(gi, bi, si + 1)

    for step in range(1, B):
        greet(gi, lax.rem(bi + step, B), si)
    for step in range(1, G // 2):
        greet(peer_grp(step), bi, si)
    greet(partner, bi, si)

    lane = lax.broadcasted_iota(jnp.int32, (R, LANES), 1)
    base, slot = plan.source(lax.broadcasted_iota(jnp.int32, (R, plan.rows), 0))
    token = lax.broadcasted_iota(jnp.int32, (R, plan.rows), 1)
    valid_row = (valid_ref[...] > 0).astype(jnp.float32)
    flag_lane = lax.broadcasted_iota(jnp.int32, (UNIT, LANES), 1)
    flags = jnp.zeros((UNIT, LANES), jnp.float32)
    for c in range(CHUNKS):
        cols = slice(c * LANES, (c + 1) * LANES)
        packed = jnp.concatenate([q_ref[:, cols], k_ref[:, cols], v_ref[:, cols]], axis=1)
        moved = []
        for half in range(2):
            h = 2 * c + half
            hit = token == base + ((slot + offs_ref[1, h]) & (plan.period - 1))
            onehot = jnp.where(hit, jnp.float32(1), jnp.float32(0))
            moved.append(jnp.dot(onehot.astype(jnp.bfloat16), packed, preferred_element_type=jnp.float32))
            column = jnp.sum(onehot * valid_row, axis=1, keepdims=True)
            for u in range(R // UNIT):
                flags = jnp.where(
                    flag_lane == u * FLAG_STRIDE + h, column[u * UNIT:(u + 1) * UNIT, :], flags
                )
        for part in range(3):
            seg = slice(part * LANES, (part + 1) * LANES)
            got = jnp.where(lane < HD, moved[0][:, seg], moved[1][:, seg])
            if part == 0:
                qs[c] = (got * 0.125).astype(jnp.bfloat16)
                continue
            got = got.astype(jnp.bfloat16)
            at = c + (part - 1) * CHUNKS
            buf_a[0, 0, 0, at] = got[:plan.starts[1]]
            buf_b[0, 0, at] = got[plan.starts[1]:plan.starts[2]]
            buf_c[0, at] = got[plan.starts[2]:]
    buf_a[0, 0, 0, 2 * CHUNKS, 0:UNIT] = flags.astype(jnp.bfloat16)

    left_side = jnp.where(si > 0, 1, 0)
    right_side = jnp.where(si < N - 1, 1, 0)
    pl.semaphore_wait(barrier, left_side + right_side + (B - 1) + (G // 2 - 1) + 1)

    def zslot(part, r):
        return (buf_a.at[0, 0, r], buf_b.at[0, r], buf_c.at[r])[part]

    def zcopy(part, r, direction):
        to = (r + 1) % N if direction == 0 else (r - 1) % N
        near = si - 1 if direction == 0 else si + 1
        return pltpu.make_async_remote_copy(
            src_ref=zslot(part, r), dst_ref=zslot(part, to),
            send_sem=zsend.at[part, r, direction], recv_sem=zrecv.at[part, to],
            device_id=(gi, bi, near), device_id_type=MESH,
        )

    def ycopy(part, r, step):
        to = B - step

        def place(x):
            return buf_a.at[0, x, r] if part == 0 else buf_b.at[x, r]

        return pltpu.make_async_remote_copy(
            src_ref=place(0), dst_ref=place(to),
            send_sem=ysend.at[part, step, r], recv_sem=yrecv.at[part, to, r],
            device_id=(gi, lax.rem(bi + step, B), si), device_id_type=MESH,
        )

    def xcopy(y, r, step):
        to = (2 * (G // 2 - step)) % G
        return pltpu.make_async_remote_copy(
            src_ref=buf_a.at[0, y, r], dst_ref=buf_a.at[to, y, r],
            send_sem=xsend.at[step, y, r], recv_sem=xrecv.at[to, y, r],
            device_id=(peer_grp(step), bi, si), device_id_type=MESH,
        )

    def fcopy(x, y, r):
        return pltpu.make_async_remote_copy(
            src_ref=buf_a.at[x, y, r], dst_ref=buf_a.at[x + 1, y, r],
            send_sem=fsend.at[x, y, r], recv_sem=xrecv.at[x + 1, y, r],
            device_id=(partner, bi, si), device_id_type=MESH,
        )

    def spread_grp(y, r):
        for step in range(1, G // 2):
            xcopy(y, r, step).start()
        fcopy(0, y, r).start()

    def spread_blk(part, r):
        for step in range(1, B):
            ycopy(part, r, step).start()

    def own_z(part):
        @pl.when(si > 0)
        def _():
            zcopy(part, 0, 0).start()

        @pl.when(si < N - 1)
        def _():
            zcopy(part, 0, 1).start()

    def arrive(part, r):
        pltpu.make_async_copy(zslot(part, r), zslot(part, r), zrecv.at[part, r]).wait()

    def take(part, d):
        @pl.when(si + d <= N - 1)
        def _():
            arrive(part, d)

            @pl.when(si > 0)
            def _():
                zcopy(part, d, 0).start()

            if part < 2:
                spread_blk(part, d)
            if part == 0:
                spread_grp(0, d)

        @pl.when(si - d >= 0)
        def _():
            arrive(part, N - d)

            @pl.when(si < N - 1)
            def _():
                zcopy(part, N - d, 1).start()

            if part < 2:
                spread_blk(part, N - d)
            if part == 0:
                spread_grp(0, N - d)

    own_z(0)
    spread_blk(0, 0)
    spread_grp(0, 0)
    own_z(1)
    spread_blk(1, 0)
    for d in range(1, N):
        take(0, d)
        take(1, d)
        if d == 1:
            own_z(2)
    for r in range(N):
        for y in range(1, B):
            ref = buf_a.at[0, y, r]
            pltpu.make_async_copy(ref, ref, yrecv.at[0, y, r]).wait()
            spread_grp(y, r)
    if N > 1:
        take(2, 1)
    for r in range(N):
        for y in range(B):
            for step in range(1, G // 2):
                ref = buf_a.at[2 * step, y, r]
                pltpu.make_async_copy(ref, ref, xrecv.at[2 * step, y, r]).wait()
                fcopy(2 * step, y, r).start()
    for d in range(2, N):
        take(2, d)

    head_pick = lax.broadcasted_iota(jnp.int32, (FLAG_STRIDE, LANES), 1) & (FLAG_STRIDE - 1)
    head_pick = head_pick == lax.broadcasted_iota(jnp.int32, (FLAG_STRIDE, LANES), 0)
    head_pick = jnp.where(head_pick, jnp.float32(1), jnp.float32(0)).astype(jnp.bfloat16)

    def gather(level, at):
        pieces = []
        for u in range(plan.units[0]):
            rows = slice(u * UNIT, (u + 1) * UNIT)
            part = (buf_a[0, 0, :, at, rows], buf_a[0, :, :, at, rows], buf_a[:, :, :, at, rows])[level]
            pieces.append(part.reshape(-1, LANES))
        if level < 2:
            for u in range(plan.units[1]):
                rows = slice(u * UNIT, (u + 1) * UNIT)
                part = buf_b[0, :, at, rows] if level == 0 else buf_b[:, :, at, rows]
                pieces.append(part.reshape(-1, LANES))
        if level == 0:
            for u in range(plan.units[2]):
                pieces.append(buf_c[:, at, u * UNIT:(u + 1) * UNIT].reshape(-1, LANES))
        return pieces[0] if len(pieces) == 1 else jnp.concatenate(pieces, axis=0)

    def level_attend(level):
        M = (R, plan.starts[2], plan.starts[1])[level]
        tiles = M // UNIT
        devices = (N, B * N, G * B * N)[level]
        per_unit = devices * UNIT
        rows = slice(0, UNIT)
        at = 2 * CHUNKS
        tall = (buf_a[0, 0, :, at, rows], buf_a[0, :, :, at, rows], buf_a[:, :, :, at, rows])[level]
        tall = tall.reshape(per_unit, LANES).astype(jnp.float32)
        unit_lane = lax.broadcasted_iota(jnp.int32, (per_unit, LANES), 1) // FLAG_STRIDE
        tall = [jnp.where(unit_lane == u, tall, 0.0).astype(jnp.bfloat16) for u in range(tiles)]
        tall = tall[0] if tiles == 1 else jnp.concatenate(tall, axis=0)
        ok = lax.dot_general(
            head_pick, tall, (((1,), (1,)), ((), ())), preferred_element_type=jnp.float32
        )
        keys = per_unit * tiles
        t = lax.broadcasted_iota(jnp.int32, (M, keys), 0)
        own = lax.broadcasted_iota(jnp.int32, (M, keys), 1) == (t // UNIT) * per_unit + (t % UNIT)
        half_lane = lax.broadcasted_iota(jnp.int32, (M, LANES), 1) < HD
        results = []
        for c in range(CHUNKS):
            q = qs[c, 0:M]
            zero = jnp.zeros_like(q)
            both = jnp.concatenate([jnp.where(half_lane, q, zero), jnp.where(half_lane, zero, q)], axis=0)
            scores = lax.dot_general(
                both, gather(level, c), (((1,), (1,)), ((), ())), preferred_element_type=jnp.float32
            )
            values = gather(level, CHUNKS + c)
            probs, tops, totals = [], [], []
            for half in range(2):
                h = 2 * c + half
                s = jnp.where(own | (ok[h:h + 1, :] > 0.5), scores[half * M:(half + 1) * M], NEG)
                top = jnp.max(s, axis=1, keepdims=True)
                weight = jnp.exp(s - top)
                totals.append(jnp.sum(weight, axis=1, keepdims=True))
                tops.append(top)
                probs.append(weight.astype(jnp.bfloat16))
            mixed = jnp.dot(jnp.concatenate(probs, axis=0), values, preferred_element_type=jnp.float32)
            mixture = jnp.where(half_lane, mixed[:M] / totals[0], mixed[M:] / totals[1])
            lse = jnp.where(half_lane, tops[0] + jnp.log(totals[0]), tops[1] + jnp.log(totals[1]))
            results.append((mixture, lse))
        return results

    first = level_attend(0)
    for r in range(N):
        for y in range(1, B):
            ref = buf_b.at[y, r]
            pltpu.make_async_copy(ref, ref, yrecv.at[1, y, r]).wait()
    second = level_attend(1)
    for r in range(N):
        for y in range(B):
            for x in range(1, G, 2):
                ref = buf_a.at[x, y, r]
                pltpu.make_async_copy(ref, ref, xrecv.at[x, y, r]).wait()
    third = level_attend(2)

    a_end, b_end = plan.starts[1], plan.starts[2]

    def combine(levels):
        top = functools.reduce(jnp.maximum, [lse for _, lse in levels])
        shares = [jnp.exp(lse - top) for _, lse in levels]
        return sum(s * o for s, (o, _) in zip(shares, levels)) / sum(shares)

    base, slot = plan.source(lax.broadcasted_iota(jnp.int32, (plan.rows, R), 1))
    token = lax.broadcasted_iota(jnp.int32, (plan.rows, R), 0)
    out_lane = lax.broadcasted_iota(jnp.int32, (plan.rows, LANES), 1)
    attention = []
    for c in range(CHUNKS):
        (o1, l1), (o2, l2), (o3, l3) = first[c], second[c], third[c]
        mixed = jnp.concatenate(
            [
                combine([(o1[:a_end], l1[:a_end]), (o2[:a_end], l2[:a_end]), (o3, l3)]),
                combine([(o1[a_end:b_end], l1[a_end:b_end]), (o2[a_end:], l2[a_end:])]),
                o1[b_end:],
            ],
            axis=0,
        ).astype(jnp.bfloat16)
        back = []
        for half in range(2):
            hit = token == base + ((slot + offs_ref[1, 2 * c + half]) & (plan.period - 1))
            onehot = jnp.where(hit, jnp.float32(1), jnp.float32(0)).astype(jnp.bfloat16)
            back.append(jnp.dot(onehot, mixed, preferred_element_type=jnp.float32))
        attention.append(jnp.where(out_lane < HD, back[0], back[1]).astype(jnp.bfloat16))
    attention = jnp.concatenate(attention, axis=1)
    o_ref[...] = jnp.dot(attention, w_ref[...], preferred_element_type=jnp.float32).astype(o_ref.dtype)

    for part in range(3):
        for r in range(N):
            goes_left = si > 0 if r == 0 else (si > 0) & (si + r <= N - 1)
            goes_right = si < N - 1 if r == 0 else (si < N - 1) & (si + r > N - 1)

            @pl.when(goes_left)
            def _():
                zcopy(part, r, 0).wait_send()

            @pl.when(goes_right)
            def _():
                zcopy(part, r, 1).wait_send()

            if part < 2:
                for step in range(1, B):
                    ycopy(part, r, step).wait_send()
            if part == 0:
                for y in range(B):
                    for step in range(1, G // 2):
                        xcopy(y, r, step).wait_send()
                    for x in range(0, G, 2):
                        fcopy(x, y, r).wait_send()


def solution(mesh):
    G, B, N = mesh.shape["grp"], mesh.shape["blk"], mesh.shape["set"]

    def per_device(queries, keys, values, valid, offsets, w_out):
        rows, width = queries.shape
        plan = Plan(G, B, N, rows)
        vmem = pl.BlockSpec(memory_space=pltpu.VMEM)
        smem = pl.BlockSpec(memory_space=pltpu.SMEM)
        dma = pltpu.SemaphoreType.DMA
        ra, rb, rc = plan.sizes
        return pl.pallas_call(
            functools.partial(kernel, plan),
            out_shape=jax.ShapeDtypeStruct((rows, w_out.shape[1]), jnp.bfloat16),
            in_specs=[vmem, vmem, vmem, vmem, smem, vmem],
            out_specs=vmem,
            scratch_shapes=[
                pltpu.VMEM((G, B, N, 2 * CHUNKS + 1, ra, LANES), jnp.bfloat16),
                pltpu.VMEM((B, N, 2 * CHUNKS, rb, LANES), jnp.bfloat16),
                pltpu.VMEM((N, 2 * CHUNKS, rc, LANES), jnp.bfloat16),
                pltpu.VMEM((CHUNKS, plan.total, LANES), jnp.bfloat16),
                dma((3, N)),
                dma((3, N, 2)),
                dma((2, B, N)),
                dma((2, B, N)),
                dma((G, B, N)),
                dma((G // 2, B, N)),
                dma((G, B, N)),
            ],
            compiler_params=pltpu.CompilerParams(
                collective_id=0, has_side_effects=True, vmem_limit_bytes=60 * 1024 * 1024
            ),
        )(queries, keys, values, valid.reshape(1, rows), offsets, w_out)

    rows_spec = P(("grp", "blk", "set"), None)
    return jax.shard_map(
        per_device,
        mesh=mesh,
        in_specs=(rows_spec, rows_spec, rows_spec, P(("grp", "blk", "set")), P(), P()),
        out_specs=rows_spec,
        check_vma=False,
    )
```

profile of v0, /device:TPU:0, one launch (start us, length us, event | category | flops | bytes accessed | tf_op | source)
XLA Modules:
  0.0 30.4 jit_solution(17619696472153112783)
XLA Ops:
  0.0 28.8 %shard_map.64 = bf16[128,768]{1,0:T(8,128)(2,1)} custom-call(bf16[128,384]{1,0:T(8,128)(2,1)} %q_ref.1, bf16[128,384]{1,0:T(8,128)(2,1)} %k_ref.1, bf16[128,384]{1,0:T(8,128)(2,1)} %v_ref.1, s32[1,128]{1,0:T(1,128)} %bitcast.1, s32[2,6]{1,0:T(2,128)} %offs_ref.1, bf16[384,768]{1,0:T(8,128)(2,1)} %w_ref.1), custom_call_target="tpu_custom_call" | custom-call | tf_op jit(solution)/shard_map/pallas_call | solution.py:379
  28.8 1.6 %copy.8 = bf16[128,768]{1,0:T(8,128)(2,1)} copy(bf16[128,768]{1,0:T(8,128)(2,1)} %shard_map.64) | data formatting | bytes 393216
where the time goes:
time: 30.6 us; the launch traced here: 30.4 us
  Pallas kernels  28.8 us (94%)
  local copies, waits for them, and re-layouts  1.62 us (5%)
    pallas_call x1, Pallas kernels, per_device(): pl.pallas_call(functools.partial(kernel, plan), out_shape=jax.ShapeDtypeS...  28.8 us
    unnamed x1, local copies, waits for them, and re-layouts  1.62 us

commit v1 on v0

v1 whole, which is shorter than its diff:
```python
import functools

import jax
import jax.numpy as jnp
from jax import lax
from jax.experimental import pallas as pl
from jax.experimental.pallas import tpu as pltpu
from jax.sharding import PartitionSpec as P

HEAD_COUNT = 6
HD = 64
LANES = 128
UNIT = 16
FLAG_STRIDE = 8
CHUNKS = HEAD_COUNT * HD // LANES
SETS = ((0, 3, 4), (2, 1, 5))
PARTS = 3
MESH = pl.DeviceIdType.MESH
NEG = -1e30


def units(count):
    return -(-count // UNIT)


def split_pow2(x, size):
    shift = size.bit_length() - 1
    return lax.shift_right_logical(x, shift), x & (size - 1)


class Plan:
    def __init__(self, grp, blk, n, rows):
        self.grp, self.blk, self.n, self.rows = grp, blk, n, rows
        self.period = grp * blk
        self.c3 = rows // self.period
        c2 = rows // blk
        self.counts = (self.c3, c2 - self.c3, rows - c2)
        self.units = tuple(units(c) for c in self.counts)
        self.sizes = tuple(u * UNIT for u in self.units)
        self.starts = (0, self.sizes[0], self.sizes[0] + self.sizes[1])
        self.total = sum(self.sizes)

    def source(self, t):
        a = t
        b = t - self.starts[1]
        c = t - self.starts[2]
        bv, bg = split_pow2(b, self.c3)
        cv, cg = split_pow2(c, self.c3)
        ck, cm = split_pow2(cv, self.grp)
        is_a = t < self.starts[1]
        is_b = t < self.starts[2]
        group = jnp.where(is_a, a, jnp.where(is_b, bg, cg))
        slot = jnp.where(is_a, 0, jnp.where(is_b, (bv + 1) * self.blk, cm * self.blk + ck + 1))
        local = jnp.where(is_a, a, jnp.where(is_b, b, c))
        count = jnp.where(is_a, self.counts[0], jnp.where(is_b, self.counts[1], self.counts[2]))
        return jnp.where(local < count, group * self.period, -(1 << 20)), slot


def flip(s, r):
    step = 1
    while step <= r:
        if r & step:
            s = s + step * (1 - 2 * ((s // step) % 2))
        step *= 2
    return s


def kernel(
    plan, q_hbm, k_hbm, v_hbm, valid_hbm, offs_hbm, w_hbm, o_ref,
    q_ref, k_ref, v_ref, valid_ref, offs_ref, w_ref,
    buf_a, buf_b, buf_c, snd_a, snd_b, snd_c, snd_q, qbuf, ret_s, ret_r, own_o, back_hot,
    load, zsend, zrecv, qsend, qrecv, asend, arecv, bsend, brecv, fsend, frecv, rsend, rrecv,
):
    G, B, N = plan.grp, plan.blk, plan.n
    R = plan.total
    K = G // 2
    gi, bi, si = lax.axis_index("grp"), lax.axis_index("blk"), lax.axis_index("set")
    core = gi % 2
    partner = gi + 1 - 2 * core
    even = si % 2 == 0

    def peer(sx, sy):
        return (lax.rem(gi + 2 * sx, G), lax.rem(bi + sy, B), si)

    across = [(sx, sy) for sx in range(K) for sy in range(B) if sx or sy]

    barrier = pltpu.get_barrier_semaphore()

    def greet(device):
        pl.semaphore_signal(barrier, inc=1, device_id=device, device_id_type=MESH)

    for r in range(N - 1, 0, -1):
        greet((gi, bi, flip(si, r)))
    for sx, sy in across:
        greet(peer(sx, sy))
    greet((partner, bi, si))

    loads = [
        pltpu.make_async_copy(src, dst, load.at[i])
        for i, (src, dst) in enumerate(
            [
                (offs_hbm, offs_ref), (valid_hbm, valid_ref), (k_hbm, k_ref),
                (v_hbm, v_ref), (q_hbm, q_ref), (w_hbm, w_ref),
            ]
        )
    ]
    for copy in loads:
        copy.start()
    for copy in loads[:5]:
        copy.wait()

    lane = lax.broadcasted_iota(jnp.int32, (R, LANES), 1)
    left = lane < HD
    base, slot = plan.source(lax.broadcasted_iota(jnp.int32, (R, plan.rows), 0))
    token = lax.broadcasted_iota(jnp.int32, (R, plan.rows), 1)
    valid_row = (valid_ref[...] > 0).astype(jnp.float32)
    flag_lane = lax.broadcasted_iota(jnp.int32, (UNIT, LANES), 1)

    moved = {}
    columns = {}
    for h in range(HEAD_COUNT):
        cols = slice((h // 2) * LANES, (h // 2 + 1) * LANES)
        packed = jnp.concatenate([q_ref[:, cols], k_ref[:, cols], v_ref[:, cols]], axis=1)
        hit = token == base + ((slot + offs_ref[1, h]) & (plan.period - 1))
        onehot = jnp.where(hit, jnp.float32(1), jnp.float32(0))
        moved[h] = jnp.dot(onehot.astype(jnp.bfloat16), packed, preferred_element_type=jnp.float32)
        columns[h] = jnp.sum(onehot * valid_row, axis=1, keepdims=True)

    def piece(h, which):
        return moved[h][:, which * LANES:(which + 1) * LANES]

    packs = []
    for number, (a, b, c) in enumerate(SETS):
        flags = jnp.zeros((UNIT, LANES), jnp.float32)
        for j, h in enumerate((a, b, c)):
            for u in range(R // UNIT):
                flags = jnp.where(
                    flag_lane == u * FLAG_STRIDE + j, columns[h][u * UNIT:(u + 1) * UNIT, :], flags
                )
        turned = pltpu.roll(piece(c, 2), HD, 1)
        mixed = jnp.where(left, piece(c, 1), turned) if number == 0 else jnp.where(left, turned, piece(c, 1))
        packs.append(
            (
                jnp.where(left, piece(a, 1), piece(b, 1)),
                jnp.where(left, piece(a, 2), piece(b, 2)),
                mixed,
                jnp.where(left, piece(a, 0), piece(b, 0)) * 0.125,
                piece(c, 0) * 0.125,
                flags,
            )
        )
    mine = [jnp.where(even, x, y).astype(jnp.bfloat16) for x, y in zip(*packs)]
    other = [jnp.where(even, y, x).astype(jnp.bfloat16) for x, y in zip(*packs)]
    a_end, b_end = plan.starts[1], plan.starts[2]
    for j in range(PARTS):
        buf_a[0, 0, 0, j] = mine[j][:a_end]
        snd_a[j] = other[j][:a_end]
        buf_b[0, 0, j] = mine[j][a_end:b_end]
        snd_b[j] = other[j][a_end:b_end]
        buf_c[0, j] = mine[j][b_end:]
        snd_c[j] = other[j][b_end:]
    buf_a[0, 0, 0, PARTS, 0:UNIT] = mine[5]
    snd_a[PARTS, 0:UNIT] = other[5]
    for j in range(2):
        qbuf[0, j] = mine[3 + j]
        snd_q[j] = other[3 + j]

    pl.semaphore_wait(barrier, (N - 1) + len(across) + 1)

    def zcopy(part, r):
        own = (buf_a.at[0, 0, 0], buf_b.at[0, 0], buf_c.at[0])[part]
        sent = (snd_a, snd_b, snd_c)[part]
        return pltpu.make_async_remote_copy(
            src_ref=sent if r % 2 else own,
            dst_ref=(buf_a.at[0, 0, r], buf_b.at[0, r], buf_c.at[r])[part],
            send_sem=zsend.at[part, r], recv_sem=zrecv.at[part, r],
            device_id=(gi, bi, flip(si, r)), device_id_type=MESH,
        )

    def qcopy():
        return pltpu.make_async_remote_copy(
            src_ref=snd_q, dst_ref=qbuf.at[1], send_sem=qsend, recv_sem=qrecv,
            device_id=(gi, bi, flip(si, 1)), device_id_type=MESH,
        )

    def acopy(sx, sy, r):
        tx, ty = 2 * ((K - sx) % K), (B - sy) % B
        return pltpu.make_async_remote_copy(
            src_ref=buf_a.at[0, 0, r], dst_ref=buf_a.at[tx, ty, r],
            send_sem=asend.at[sx, sy, r], recv_sem=arecv.at[tx // 2, ty, r],
            device_id=peer(sx, sy), device_id_type=MESH,
        )

    def bcopy(sy, r):
        return pltpu.make_async_remote_copy(
            src_ref=buf_b.at[0, r], dst_ref=buf_b.at[B - sy, r],
            send_sem=bsend.at[sy, r], recv_sem=brecv.at[B - sy, r],
            device_id=peer(0, sy), device_id_type=MESH,
        )

    def fcopy(x, y):
        return pltpu.make_async_remote_copy(
            src_ref=buf_a.at[2 * x, y], dst_ref=buf_a.at[2 * x + 1, y],
            send_sem=fsend.at[x, y], recv_sem=frecv.at[x, y],
            device_id=(partner, bi, si), device_id_type=MESH,
        )

    def rcopy(j):
        return pltpu.make_async_remote_copy(
            src_ref=ret_s.at[j], dst_ref=ret_r.at[j], send_sem=rsend.at[j], recv_sem=rrecv.at[j],
            device_id=(gi, bi, flip(si, 1)), device_id_type=MESH,
        )

    def spread_a(r):
        for sx, sy in across:
            acopy(sx, sy, r).start()

    def spread_b(r):
        for sy in range(1, B):
            bcopy(sy, r).start()

    order = list(range(N - 1, 0, -1))
    for r in order:
        zcopy(0, r).start()
    spread_a(0)
    for r in order:
        zcopy(1, r).start()
    spread_b(0)
    for r in order[:-1]:
        zcopy(2, r).start()
    if N > 1:
        qcopy().start()
        zcopy(2, 1).start()

    token = lax.broadcasted_iota(jnp.int32, (plan.rows, R), 0)
    base, slot = plan.source(lax.broadcasted_iota(jnp.int32, (plan.rows, R), 1))
    for h in range(HEAD_COUNT):
        hit = token == base + ((slot + offs_ref[1, h]) & (plan.period - 1))
        back_hot[h] = jnp.where(hit, jnp.float32(1), jnp.float32(0)).astype(jnp.bfloat16)

    for r in range(1, N):
        zcopy(0, r).wait_recv()
        spread_a(r)
    fcopy(0, 0).start()
    for r in range(1, N):
        zcopy(1, r).wait_recv()
        spread_b(r)
    for sx, sy in across:
        for r in range(N):
            acopy((K - sx) % K, (B - sy) % B, r).wait_recv()
        fcopy(sx, sy).start()

    head_pick = lax.broadcasted_iota(jnp.int32, (FLAG_STRIDE, LANES), 1) & (FLAG_STRIDE - 1)
    head_pick = head_pick == lax.broadcasted_iota(jnp.int32, (FLAG_STRIDE, LANES), 0)
    head_pick = jnp.where(head_pick, jnp.float32(1), jnp.float32(0)).astype(jnp.bfloat16)

    def gather(level, at):
        pieces = []
        for u in range(plan.units[0]):
            rows = slice(u * UNIT, (u + 1) * UNIT)
            part = (buf_a[0, 0, :, at, rows], buf_a[0, :, :, at, rows], buf_a[:, :, :, at, rows])[level]
            pieces.append(part.reshape(-1, LANES))
        if level < 2:
            for u in range(plan.units[1]):
                rows = slice(u * UNIT, (u + 1) * UNIT)
                part = buf_b[0, :, at, rows] if level == 0 else buf_b[:, :, at, rows]
                pieces.append(part.reshape(-1, LANES))
        if level == 0:
            for u in range(plan.units[2]):
                pieces.append(buf_c[:, at, u * UNIT:(u + 1) * UNIT].reshape(-1, LANES))
        return pieces[0] if len(pieces) == 1 else jnp.concatenate(pieces, axis=0)

    def level_attend(level):
        M = (R, b_end, a_end)[level]
        tiles = M // UNIT
        devices = (N, B * N, G * B * N)[level]
        per_unit = devices * UNIT
        rows = slice(0, UNIT)
        at = PARTS
        tall = (buf_a[0, 0, :, at, rows], buf_a[0, :, :, at, rows], buf_a[:, :, :, at, rows])[level]
        tall = tall.reshape(per_unit, LANES).astype(jnp.float32)
        unit_lane = lax.broadcasted_iota(jnp.int32, (per_unit, LANES), 1) // FLAG_STRIDE
        tall = [jnp.where(unit_lane == u, tall, 0.0).astype(jnp.bfloat16) for u in range(tiles)]
        tall = tall[0] if tiles == 1 else jnp.concatenate(tall, axis=0)
        ok = lax.dot_general(
            head_pick, tall, (((1,), (1,)), ((), ())), preferred_element_type=jnp.float32
        )
        keys = per_unit * tiles
        t = lax.broadcasted_iota(jnp.int32, (M, keys), 0)
        spot = lax.broadcasted_iota(jnp.int32, (M, keys), 1) - ((t // UNIT) * per_unit + (t % UNIT))
        half_lane = lax.broadcasted_iota(jnp.int32, (M, LANES), 1) < HD
        value_lane = half_lane != even

        def softmax(scores, j, who):
            s = jnp.where((spot == who * UNIT) | (ok[j:j + 1, :] > 0.5), scores, NEG)
            top = jnp.max(s, axis=1, keepdims=True)
            weight = jnp.exp(s - top)
            return weight.astype(jnp.bfloat16), top, jnp.sum(weight, axis=1, keepdims=True)

        contract = (((1,), (1,)), ((), ()))
        pair_k, pair_v, single = gather(level, 0), gather(level, 1), gather(level, 2)
        zero = jnp.zeros((M, LANES), jnp.bfloat16)
        results = [[None, None], [None, None]]
        for who in (1, 0):
            q = qbuf[who, 0, 0:M]
            both = jnp.concatenate([jnp.where(half_lane, q, zero), jnp.where(half_lane, zero, q)], axis=0)
            scores = lax.dot_general(both, pair_k, contract, preferred_element_type=jnp.float32)
            weights = [softmax(scores[j * M:(j + 1) * M], j, who) for j in range(2)]
            mixed = jnp.dot(
                jnp.concatenate([w[0] for w in weights], axis=0), pair_v, preferred_element_type=jnp.float32
            )
            results[who][0] = (
                jnp.where(half_lane, mixed[:M] / weights[0][2], mixed[M:] / weights[1][2]),
                jnp.where(
                    half_lane,
                    weights[0][1] + jnp.log(weights[0][2]),
                    weights[1][1] + jnp.log(weights[1][2]),
                ),
            )
        for who in (1, 0):
            q = jnp.where(value_lane, zero, qbuf[who, 1, 0:M])
            scores = lax.dot_general(q, single, contract, preferred_element_type=jnp.float32)
            weight, top, total = softmax(scores, 2, who)
            mixed = jnp.dot(weight, single, preferred_element_type=jnp.float32)
            results[who][1] = (mixed / total, jnp.broadcast_to(top + jnp.log(total), (M, LANES)))
        return results

    if N > 1:
        qcopy().wait_recv()
    for r in range(1, N):
        zcopy(2, r).wait_recv()
    first = level_attend(0)
    for x in range(K):
        for y in range(B):
            fcopy(x, y).wait_recv()
    third = level_attend(2)
    for sy in range(1, B):
        for r in range(N):
            bcopy(B - sy, r).wait_recv()
    second = level_attend(1)

    def combine(levels):
        top = functools.reduce(jnp.maximum, [lse for _, lse in levels])
        shares = [jnp.exp(lse - top) for _, lse in levels]
        return sum(s * o for s, (o, _) in zip(shares, levels)) / sum(shares)

    for who in (1, 0):
        for j in range(2):
            (o1, l1), (o2, l2), (o3, l3) = first[who][j], second[who][j], third[who][j]
            mixed = jnp.concatenate(
                [
                    combine([(o1[:a_end], l1[:a_end]), (o2[:a_end], l2[:a_end]), (o3, l3)]),
                    combine([(o1[a_end:b_end], l1[a_end:b_end]), (o2[a_end:], l2[a_end:])]),
                    o1[b_end:],
                ],
                axis=0,
            ).astype(jnp.bfloat16)
            if who == 1:
                ret_s[j] = mixed
                rcopy(j).start()
            else:
                own_o[j] = mixed
    loads[5].wait()
    for j in range(2):
        rcopy(j).wait_recv()

    sets = [
        (jnp.where(even, own_o[j], ret_r[j]), jnp.where(even, ret_r[j], own_o[j])) for j in range(2)
    ]
    (zero_pair, one_pair), (zero_single, one_single) = sets
    singles = jnp.where(left, one_single, zero_single)
    out_left = lax.broadcasted_iota(jnp.int32, (plan.rows, LANES), 1) < HD
    attention, weights = [], []
    for value, (a, b) in ((zero_pair, SETS[0][:2]), (one_pair, SETS[1][:2]), (singles, (SETS[1][2], SETS[0][2]))):
        back = [jnp.dot(back_hot[h], value, preferred_element_type=jnp.float32) for h in (a, b)]
        attention.append(jnp.where(out_left, back[0], back[1]).astype(jnp.bfloat16))
        weights += [w_ref[a * HD:(a + 1) * HD, :], w_ref[b * HD:(b + 1) * HD, :]]
    attention = jnp.concatenate(attention, axis=1)
    weights = jnp.concatenate(weights, axis=0)
    o_ref[...] = jnp.dot(attention, weights, preferred_element_type=jnp.float32).astype(o_ref.dtype)

    for r in range(1, N):
        for part in range(3):
            zcopy(part, r).wait_send()
    if N > 1:
        qcopy().wait_send()
    for r in range(N):
        for sx, sy in across:
            acopy(sx, sy, r).wait_send()
        for sy in range(1, B):
            bcopy(sy, r).wait_send()
    for x in range(K):
        for y in range(B):
            fcopy(x, y).wait_send()
    for j in range(2):
        rcopy(j).wait_send()


def solution(mesh):
    G, B, N = mesh.shape["grp"], mesh.shape["blk"], mesh.shape["set"]

    def per_device(queries, keys, values, valid, offsets, w_out):
        rows, width = queries.shape
        plan = Plan(G, B, N, rows)
        vmem = pl.BlockSpec(memory_space=pltpu.VMEM)
        anywhere = pl.BlockSpec(memory_space=pl.ANY)
        dma = pltpu.SemaphoreType.DMA
        ra, rb, rc = plan.sizes
        R = plan.total
        bf16 = jnp.bfloat16
        return pl.pallas_call(
            functools.partial(kernel, plan),
            out_shape=jax.ShapeDtypeStruct((rows, w_out.shape[1]), bf16),
            in_specs=[anywhere] * 6,
            out_specs=vmem,
            scratch_shapes=[
                pltpu.VMEM((rows, width), bf16),
                pltpu.VMEM((rows, width), bf16),
                pltpu.VMEM((rows, width), bf16),
                pltpu.VMEM((1, rows), jnp.int32),
                pltpu.SMEM(offsets.shape, jnp.int32),
                pltpu.VMEM(w_out.shape, bf16),
                pltpu.VMEM((G, B, N, PARTS + 1, ra, LANES), bf16),
                pltpu.VMEM((B, N, PARTS, rb, LANES), bf16),
                pltpu.VMEM((N, PARTS, rc, LANES), bf16),
                pltpu.VMEM((PARTS + 1, ra, LANES), bf16),
                pltpu.VMEM((PARTS, rb, LANES), bf16),
                pltpu.VMEM((PARTS, rc, LANES), bf16),
                pltpu.VMEM((2, R, LANES), bf16),
                pltpu.VMEM((2, 2, R, LANES), bf16),
                pltpu.VMEM((2, R, LANES), bf16),
                pltpu.VMEM((2, R, LANES), bf16),
                pltpu.VMEM((2, R, LANES), bf16),
                pltpu.VMEM((HEAD_COUNT, rows, R), bf16),
                dma((6,)),
                dma((3, N)),
                dma((3, N)),
                dma,
                dma,
                dma((G // 2, B, N)),
                dma((G // 2, B, N)),
                dma((B, N)),
                dma((B, N)),
                dma((G // 2, B)),
                dma((G // 2, B)),
                dma((2,)),
                dma((2,)),
            ],
            compiler_params=pltpu.CompilerParams(
                collective_id=0, has_side_effects=True, vmem_limit_bytes=60 * 1024 * 1024
            ),
        )(queries, keys, values, valid.reshape(1, rows), offsets, w_out)

    rows_spec = P(("grp", "blk", "set"), None)
    return jax.shard_map(
        per_device,
        mesh=mesh,
        in_specs=(rows_spec, rows_spec, rows_spec, P(("grp", "blk", "set")), P(), P()),
        out_specs=rows_spec,
        check_vma=False,
    )
```

time: 30.6 us -> 25.3 us (0.83)
  Pallas kernels: 28.8 us -> 23.5 us
    pallas_call x1, Pallas kernels: 28.8 us -> 23.5 us  [per_device(): pl.pallas_call(functools.partial(kernel, plan), out_shape=jax.ShapeDtypeS...]
where the time goes in v1:
time: 25.3 us; the launch traced here: 25.2 us
  Pallas kernels  23.5 us (93%)
  local copies, waits for them, and re-layouts  1.62 us (6%)
    pallas_call x1, Pallas kernels, per_device(): pl.pallas_call(functools.partial(kernel, plan), out_shape=jax.ShapeDtypeS...  23.5 us
    unnamed x1, local copies, waits for them, and re-layouts  1.62 us

profile of v1, /device:TPU:0, one launch (start us, length us, event | category | flops | bytes accessed | tf_op | source)
XLA Modules:
  0.0 25.2 jit_solution(13445535274041874781)
XLA Ops:
  0.0 23.5 %shard_map.64 = bf16[128,768]{1,0:T(8,128)(2,1)} custom-call(bf16[128,384]{1,0:T(8,128)(2,1)} %q_hbm.1, bf16[128,384]{1,0:T(8,128)(2,1)} %k_hbm.1, bf16[128,384]{1,0:T(8,128)(2,1)} %v_hbm.1, s32[1,128]{1,0:T(1,128)} %bitcast.1, s32[2,6]{1,0:T(2,128)} %offs_hbm.1, bf16[384,768]{1,0:T(8,128)(2,1)} %w_hbm.1), custom_call_target="tpu_custom_call" | custom-call | tf_op jit(solution)/shard_map/pallas_call | solution.py:411
  23.5 1.6 %copy.8 = bf16[128,768]{1,0:T(8,128)(2,1)} copy(bf16[128,768]{1,0:T(8,128)(2,1)} %shard_map.64) | data formatting | bytes 393216

commit v2 on v1

--- a/solution.py
+++ b/solution.py
@@ -39,6 +39,7 @@
         self.sizes = tuple(u * UNIT for u in self.units)
         self.starts = (0, self.sizes[0], self.sizes[0] + self.sizes[1])
         self.total = sum(self.sizes)
+        self.half = units(-(-self.total // 2)) * UNIT
 
     def source(self, t):
         a = t
@@ -67,13 +68,14 @@
 
 def kernel(
     plan, q_hbm, k_hbm, v_hbm, valid_hbm, offs_hbm, w_hbm, o_ref,
-    q_ref, k_ref, v_ref, valid_ref, offs_ref, w_ref,
-    buf_a, buf_b, buf_c, snd_a, snd_b, snd_c, snd_q, qbuf, ret_s, ret_r, own_o, back_hot,
-    load, zsend, zrecv, qsend, qrecv, asend, arecv, bsend, brecv, fsend, frecv, rsend, rrecv,
+    qkv_ref, valid_ref, offs_ref, w_ref,
+    buf_a, buf_b, buf_c, snd_a, snd_b, snd_c, snd_q, own_q, got_q, ret_s, ret_r, own_o, back_hot,
+    load, zsend, zrecv, crecv, qsem, asend, arecv, bsend, brecv, fsend, frecv, rsem,
 ):
     G, B, N = plan.grp, plan.blk, plan.n
     R = plan.total
     K = G // 2
+    H = plan.half
     gi, bi, si = lax.axis_index("grp"), lax.axis_index("blk"), lax.axis_index("set")
     core = gi % 2
     partner = gi + 1 - 2 * core
@@ -81,6 +83,7 @@
 
     def peer(sx, sy):
         return (lax.rem(gi + 2 * sx, G), lax.rem(bi + sy, B), si)
+
 
     across = [(sx, sy) for sx in range(K) for sy in range(B) if sx or sy]
 
@@ -95,19 +98,15 @@
         greet(peer(sx, sy))
     greet((partner, bi, si))
 
-    loads = [
-        pltpu.make_async_copy(src, dst, load.at[i])
-        for i, (src, dst) in enumerate(
-            [
-                (offs_hbm, offs_ref), (valid_hbm, valid_ref), (k_hbm, k_ref),
-                (v_hbm, v_ref), (q_hbm, q_ref), (w_hbm, w_ref),
-            ]
-        )
-    ]
-    for copy in loads:
+    load_offs = pltpu.make_async_copy(offs_hbm, offs_ref, load.at[0])
+    load_valid = pltpu.make_async_copy(valid_hbm, valid_ref, load.at[1])
+    load_qkv = [pltpu.make_async_copy(src, qkv_ref.at[n], load.at[2]) for n, src in enumerate((q_hbm, k_hbm, v_hbm))]
+    load_w = pltpu.make_async_copy(w_hbm, w_ref, load.at[3])
+    for copy in (load_offs, load_valid, *load_qkv, load_w):
         copy.start()
-    for copy in loads[:5]:
-        copy.wait()
+    load_offs.wait()
+    load_valid.wait()
+    pltpu.make_async_copy(qkv_ref, qkv_ref, load.at[2]).wait()
 
     lane = lax.broadcasted_iota(jnp.int32, (R, LANES), 1)
     left = lane < HD
@@ -120,7 +119,7 @@
     columns = {}
     for h in range(HEAD_COUNT):
         cols = slice((h // 2) * LANES, (h // 2 + 1) * LANES)
-        packed = jnp.concatenate([q_ref[:, cols], k_ref[:, cols], v_ref[:, cols]], axis=1)
+        packed = jnp.concatenate([qkv_ref[n, :, cols] for n in range(3)], axis=1)
         hit = token == base + ((slot + offs_ref[1, h]) & (plan.period - 1))
         onehot = jnp.where(hit, jnp.float32(1), jnp.float32(0))
         moved[h] = jnp.dot(onehot.astype(jnp.bfloat16), packed, preferred_element_type=jnp.float32)
@@ -128,6 +127,16 @@
 
     def piece(h, which):
         return moved[h][:, which * LANES:(which + 1) * LANES]
+
+    def fold(x, keep):
+        low = x[H:]
+        if R < 2 * H:
+            low = jnp.concatenate([low, jnp.zeros((2 * H - R, LANES), low.dtype)], axis=0)
+        return jnp.where(keep, x[:H], pltpu.roll(low, HD, 1))
+
+    def unfold(x):
+        x = x.astype(jnp.float32)
+        return jnp.concatenate([x, pltpu.roll(x, HD, 1)[:R - H]], axis=0).astype(jnp.bfloat16)
 
     packs = []
     for number, (a, b, c) in enumerate(SETS):
@@ -147,6 +156,7 @@
                 jnp.where(left, piece(a, 0), piece(b, 0)) * 0.125,
                 piece(c, 0) * 0.125,
                 flags,
+                fold(piece(c, 0) * 0.125, left[:H] if number == 0 else ~left[:H]),
             )
         )
     mine = [jnp.where(even, x, y).astype(jnp.bfloat16) for x, y in zip(*packs)]
@@ -162,75 +172,101 @@
     buf_a[0, 0, 0, PARTS, 0:UNIT] = mine[5]
     snd_a[PARTS, 0:UNIT] = other[5]
     for j in range(2):
-        qbuf[0, j] = mine[3 + j]
-        snd_q[j] = other[3 + j]
+        own_q[j] = mine[3 + j]
+    snd_q[0:R] = other[3]
+    snd_q[R:R + H] = other[6]
 
     pl.semaphore_wait(barrier, (N - 1) + len(across) + 1)
 
+    heads = (slice(0, 2), slice(2, 3))
+    line_sem = (lambda r: zrecv.at[0, r - 1], lambda r: zrecv.at[1, r - 1], lambda r: zrecv.at[2, r - 1])
+
+    def line_ref(part, r):
+        if part == 0:
+            return buf_a.at[0, 0, r]
+        if part < 3:
+            return buf_b.at[0, r, heads[part - 1]]
+        return buf_c.at[r, heads[part - 3]]
+
     def zcopy(part, r):
-        own = (buf_a.at[0, 0, 0], buf_b.at[0, 0], buf_c.at[0])[part]
-        sent = (snd_a, snd_b, snd_c)[part]
+        sent = snd_a if part == 0 else (snd_b if part < 3 else snd_c).at[heads[(part - 1) % 2]]
         return pltpu.make_async_remote_copy(
-            src_ref=sent if r % 2 else own,
-            dst_ref=(buf_a.at[0, 0, r], buf_b.at[0, r], buf_c.at[r])[part],
-            send_sem=zsend.at[part, r], recv_sem=zrecv.at[part, r],
+            src_ref=sent if r % 2 else line_ref(part, 0),
+            dst_ref=line_ref(part, r),
+            send_sem=zsend.at[part],
+            recv_sem=line_sem[part](r) if part < 3 else crecv.at[part - 3],
             device_id=(gi, bi, flip(si, r)), device_id_type=MESH,
         )
+
+    def line_sent(part):
+        rest = slice(1, N)
+        ref = (
+            buf_a.at[0, 0, rest] if part == 0
+            else buf_b.at[0, rest, heads[part - 1]] if part < 3
+            else buf_c.at[rest, heads[part - 3]]
+        )
+        pltpu.make_async_copy(ref, ref, zsend.at[part]).wait()
 
     def qcopy():
         return pltpu.make_async_remote_copy(
-            src_ref=snd_q, dst_ref=qbuf.at[1], send_sem=qsend, recv_sem=qrecv,
+            src_ref=snd_q, dst_ref=got_q, send_sem=qsem.at[0], recv_sem=qsem.at[1],
             device_id=(gi, bi, flip(si, 1)), device_id_type=MESH,
         )
 
-    def acopy(sx, sy, r):
-        tx, ty = 2 * ((K - sx) % K), (B - sy) % B
+    def acopy(x, y, r):
         return pltpu.make_async_remote_copy(
-            src_ref=buf_a.at[0, 0, r], dst_ref=buf_a.at[tx, ty, r],
-            send_sem=asend.at[sx, sy, r], recv_sem=arecv.at[tx // 2, ty, r],
-            device_id=peer(sx, sy), device_id_type=MESH,
-        )
-
-    def bcopy(sy, r):
+            src_ref=buf_a.at[0, 0, r], dst_ref=buf_a.at[2 * x, y, r],
+            send_sem=asend.at[x, y], recv_sem=arecv.at[x, y],
+            device_id=peer((K - x) % K, (B - y) % B), device_id_type=MESH,
+        )
+
+    def bcopy(y, r, j):
         return pltpu.make_async_remote_copy(
-            src_ref=buf_b.at[0, r], dst_ref=buf_b.at[B - sy, r],
-            send_sem=bsend.at[sy, r], recv_sem=brecv.at[B - sy, r],
-            device_id=peer(0, sy), device_id_type=MESH,
+            src_ref=buf_b.at[0, r, heads[j]], dst_ref=buf_b.at[y, r, heads[j]],
+            send_sem=bsend.at[j, y - 1], recv_sem=brecv.at[j, y - 1],
+            device_id=peer(0, B - y), device_id_type=MESH,
         )
 
     def fcopy(x, y):
         return pltpu.make_async_remote_copy(
             src_ref=buf_a.at[2 * x, y], dst_ref=buf_a.at[2 * x + 1, y],
-            send_sem=fsend.at[x, y], recv_sem=frecv.at[x, y],
+            send_sem=fsend.at[x], recv_sem=frecv.at[x],
             device_id=(partner, bi, si), device_id_type=MESH,
         )
 
     def rcopy(j):
+        rows = (slice(0, R), slice(R, R + H))[j]
         return pltpu.make_async_remote_copy(
-            src_ref=ret_s.at[j], dst_ref=ret_r.at[j], send_sem=rsend.at[j], recv_sem=rrecv.at[j],
+            src_ref=ret_s.at[rows], dst_ref=ret_r.at[rows], send_sem=rsem.at[0, j], recv_sem=rsem.at[1, j],
             device_id=(gi, bi, flip(si, 1)), device_id_type=MESH,
         )
 
+    def arrived(ref, sem):
+        pltpu.make_async_copy(ref, ref, sem).wait()
+
     def spread_a(r):
-        for sx, sy in across:
-            acopy(sx, sy, r).start()
-
-    def spread_b(r):
-        for sy in range(1, B):
-            bcopy(sy, r).start()
+        for x, y in across:
+            acopy(x, y, r).start()
+
+    def spread_b(r, j):
+        for y in range(1, B):
+            bcopy(y, r, j).start()
 
     order = list(range(N - 1, 0, -1))
-    for r in order:
-        zcopy(0, r).start()
+
+    def send_line(part):
+        for r in order:
+            zcopy(part, r).start()
+
+    send_line(0)
     spread_a(0)
-    for r in order:
-        zcopy(1, r).start()
-    spread_b(0)
-    for r in order[:-1]:
-        zcopy(2, r).start()
-    if N > 1:
-        qcopy().start()
-        zcopy(2, 1).start()
+    send_line(1)
+    spread_b(0, 0)
+    send_line(2)
+    spread_b(0, 1)
+    qcopy().start()
+    send_line(3)
+    send_line(4)
 
     token = lax.broadcasted_iota(jnp.int32, (plan.rows, R), 0)
     base, slot = plan.source(lax.broadcasted_iota(jnp.int32, (plan.rows, R), 1))
@@ -244,11 +280,13 @@
     fcopy(0, 0).start()
     for r in range(1, N):
         zcopy(1, r).wait_recv()
-        spread_b(r)
-    for sx, sy in across:
-        for r in range(N):
-            acopy((K - sx) % K, (B - sy) % B, r).wait_recv()
-        fcopy(sx, sy).start()
+        spread_b(r, 0)
+    for r in range(1, N):
+        zcopy(2, r).wait_recv()
+        spread_b(r, 1)
+    for x, y in across:
+        arrived(buf_a.at[2 * x, y], arecv.at[x, y])
+        fcopy(x, y).start()
 
     head_pick = lax.broadcasted_iota(jnp.int32, (FLAG_STRIDE, LANES), 1) & (FLAG_STRIDE - 1)
     head_pick = head_pick == lax.broadcasted_iota(jnp.int32, (FLAG_STRIDE, LANES), 0)
@@ -286,67 +324,78 @@
             head_pick, tall, (((1,), (1,)), ((), ())), preferred_element_type=jnp.float32
         )
         keys = per_unit * tiles
-        t = lax.broadcasted_iota(jnp.int32, (M, keys), 0)
-        spot = lax.broadcasted_iota(jnp.int32, (M, keys), 1) - ((t // UNIT) * per_unit + (t % UNIT))
-        half_lane = lax.broadcasted_iota(jnp.int32, (M, LANES), 1) < HD
+        row = lax.broadcasted_iota(jnp.int32, (2 * M, keys), 0)
+        who = jnp.where(row < M, 0, 1)
+        t = row - who * M
+        spot = (t // UNIT) * per_unit + (t % UNIT) + who * UNIT
+        own = lax.broadcasted_iota(jnp.int32, (2 * M, keys), 1) == spot
+        half_lane = lax.broadcasted_iota(jnp.int32, (2 * M, LANES), 1) < HD
         value_lane = half_lane != even
-
-        def softmax(scores, j, who):
-            s = jnp.where((spot == who * UNIT) | (ok[j:j + 1, :] > 0.5), scores, NEG)
-            top = jnp.max(s, axis=1, keepdims=True)
-            weight = jnp.exp(s - top)
-            return weight.astype(jnp.bfloat16), top, jnp.sum(weight, axis=1, keepdims=True)
-
         contract = (((1,), (1,)), ((), ()))
-        pair_k, pair_v, single = gather(level, 0), gather(level, 1), gather(level, 2)
-        zero = jnp.zeros((M, LANES), jnp.bfloat16)
-        results = [[None, None], [None, None]]
-        for who in (1, 0):
-            q = qbuf[who, 0, 0:M]
-            both = jnp.concatenate([jnp.where(half_lane, q, zero), jnp.where(half_lane, zero, q)], axis=0)
-            scores = lax.dot_general(both, pair_k, contract, preferred_element_type=jnp.float32)
-            weights = [softmax(scores[j * M:(j + 1) * M], j, who) for j in range(2)]
-            mixed = jnp.dot(
-                jnp.concatenate([w[0] for w in weights], axis=0), pair_v, preferred_element_type=jnp.float32
-            )
-            results[who][0] = (
-                jnp.where(half_lane, mixed[:M] / weights[0][2], mixed[M:] / weights[1][2]),
-                jnp.where(
-                    half_lane,
-                    weights[0][1] + jnp.log(weights[0][2]),
-                    weights[1][1] + jnp.log(weights[1][2]),
-                ),
-            )
-        for who in (1, 0):
-            q = jnp.where(value_lane, zero, qbuf[who, 1, 0:M])
-            scores = lax.dot_general(q, single, contract, preferred_element_type=jnp.float32)
-            weight, top, total = softmax(scores, 2, who)
-            mixed = jnp.dot(weight, single, preferred_element_type=jnp.float32)
-            results[who][1] = (mixed / total, jnp.broadcast_to(top + jnp.log(total), (M, LANES)))
-        return results
-
-    if N > 1:
-        qcopy().wait_recv()
-    for r in range(1, N):
-        zcopy(2, r).wait_recv()
-    first = level_attend(0)
-    for x in range(K):
-        for y in range(B):
-            fcopy(x, y).wait_recv()
-    third = level_attend(2)
-    for sy in range(1, B):
-        for r in range(N):
-            bcopy(B - sy, r).wait_recv()
-    second = level_attend(1)
+        zero = jnp.zeros((2 * M, LANES), jnp.bfloat16)
+
+        def query(j):
+            return jnp.concatenate([own_q[j, 0:M], got_q[0:M] if j == 0 else got_single[0:M]], axis=0)
+
+        def run(parts):
+            scores = []
+            if 0 in parts:
+                q = query(0)
+                both = jnp.concatenate([jnp.where(half_lane, q, zero), jnp.where(half_lane, zero, q)], axis=0)
+                both = lax.dot_general(both, gather(level, 0), contract, preferred_element_type=jnp.float32)
+                scores += [both[:2 * M], both[2 * M:]]
+            if 1 in parts:
+                single = gather(level, 2)
+                q = jnp.where(value_lane, zero, query(1))
+                scores.append(lax.dot_general(q, single, contract, preferred_element_type=jnp.float32))
+            first = 0 if 0 in parts else 2
+            scores = [jnp.where(own | (ok[first + n:first + n + 1, :] > 0.5), s, NEG) for n, s in enumerate(scores)]
+            tops = [jnp.max(s, axis=1, keepdims=True) for s in scores]
+            weights = [jnp.exp(s - top) for s, top in zip(scores, tops)]
+            probs = [w.astype(jnp.bfloat16) for w in weights]
+            results = []
+            if 0 in parts:
+                pair = jnp.dot(jnp.concatenate(probs[:2], axis=0), gather(level, 1), preferred_element_type=jnp.float32)
+            if 1 in parts:
+                alone = jnp.dot(probs[-1], single, preferred_element_type=jnp.float32)
+            totals = [jnp.sum(w, axis=1, keepdims=True) for w in weights]
+            lses = [top + jnp.log(total) for top, total in zip(tops, totals)]
+            if 0 in parts:
+                results.append(
+                    (
+                        jnp.where(half_lane, pair[:2 * M] / totals[0], pair[2 * M:] / totals[1]),
+                        jnp.where(half_lane, lses[0], lses[1]),
+                    )
+                )
+            if 1 in parts:
+                results.append((alone / totals[-1], jnp.broadcast_to(lses[-1], (2 * M, LANES))))
+            return results
+
+        return run
 
     def combine(levels):
         top = functools.reduce(jnp.maximum, [lse for _, lse in levels])
         shares = [jnp.exp(lse - top) for _, lse in levels]
         return sum(s * o for s, (o, _) in zip(shares, levels)) / sum(shares)
 
-    for who in (1, 0):
-        for j in range(2):
-            (o1, l1), (o2, l2), (o3, l3) = first[who][j], second[who][j], third[who][j]
+    qcopy().wait_recv()
+    for x in range(K):
+        arrived(buf_a.at[2 * x + 1], frecv.at[x])
+    got_single = unfold(got_q[R:R + H])
+    outer, middle, dense = level_attend(2), level_attend(1), level_attend(0)
+    third = outer((0, 1))
+    value_half = left[:H] != even
+    for j in range(2):
+        for y in range(1, B):
+            arrived(buf_b.at[y, :, heads[j]], brecv.at[j, y - 1])
+        second = middle((j,))[0]
+        arrived(buf_c.at[1:N, heads[j]], crecv.at[j])
+        first = dense((j,))[0]
+        for who in (1, 0):
+            (o1, l1), (o2, l2), (o3, l3) = [
+                tuple(x[who * m:(who + 1) * m] for x in level)
+                for level, m in ((first, R), (second, b_end), (third[j], a_end))
+            ]
             mixed = jnp.concatenate(
                 [
                     combine([(o1[:a_end], l1[:a_end]), (o2[:a_end], l2[:a_end]), (o3, l3)]),
@@ -354,18 +403,32 @@
                     o1[b_end:],
                 ],
                 axis=0,
-            ).astype(jnp.bfloat16)
-            if who == 1:
-                ret_s[j] = mixed
+            )
+            if who == 0:
+                own_o[j] = mixed.astype(jnp.bfloat16)
+            else:
+                if j == 0:
+                    ret_s[0:R] = mixed.astype(jnp.bfloat16)
+                else:
+                    ret_s[R:R + H] = fold(mixed, value_half).astype(jnp.bfloat16)
                 rcopy(j).start()
-            else:
-                own_o[j] = mixed
-    loads[5].wait()
+    for part in range(5):
+        line_sent(part)
+    qcopy().wait_send()
+    for x, y in across:
+        arrived(buf_a.at[0, 0], asend.at[x, y])
+    for j in range(2):
+        for y in range(1, B):
+            arrived(buf_b.at[0, :, heads[j]], bsend.at[j, y - 1])
+    for x in range(K):
+        arrived(buf_a.at[2 * x], fsend.at[x])
+    load_w.wait()
     for j in range(2):
         rcopy(j).wait_recv()
 
+    got = (ret_r[0:R], unfold(ret_r[R:R + H]))
     sets = [
-        (jnp.where(even, own_o[j], ret_r[j]), jnp.where(even, ret_r[j], own_o[j])) for j in range(2)
+        (jnp.where(even, own_o[j], got[j]), jnp.where(even, got[j], own_o[j])) for j in range(2)
     ]
     (zero_pair, one_pair), (zero_single, one_single) = sets
     singles = jnp.where(left, one_single, zero_single)
@@ -379,19 +442,6 @@
     weights = jnp.concatenate(weights, axis=0)
     o_ref[...] = jnp.dot(attention, weights, preferred_element_type=jnp.float32).astype(o_ref.dtype)
 
-    for r in range(1, N):
-        for part in range(3):
-            zcopy(part, r).wait_send()
-    if N > 1:
-        qcopy().wait_send()
-    for r in range(N):
-        for sx, sy in across:
-            acopy(sx, sy, r).wait_send()
-        for sy in range(1, B):
-            bcopy(sy, r).wait_send()
-    for x in range(K):
-        for y in range(B):
-            fcopy(x, y).wait_send()
     for j in range(2):
         rcopy(j).wait_send()
 
@@ -414,9 +464,7 @@
             in_specs=[anywhere] * 6,
             out_specs=vmem,
             scratch_shapes=[
-                pltpu.VMEM((rows, width), bf16),
-                pltpu.VMEM((rows, width), bf16),
-                pltpu.VMEM((rows, width), bf16),
+                pltpu.VMEM((3, rows, width), bf16),
                 pltpu.VMEM((1, rows), jnp.int32),
                 pltpu.SMEM(offsets.shape, jnp.int32),
                 pltpu.VMEM(w_out.shape, bf16),
@@ -426,25 +474,25 @@
                 pltpu.VMEM((PARTS + 1, ra, LANES), bf16),
                 pltpu.VMEM((PARTS, rb, LANES), bf16),
                 pltpu.VMEM((PARTS, rc, LANES), bf16),
+                pltpu.VMEM((R + plan.half, LANES), bf16),
                 pltpu.VMEM((2, R, LANES), bf16),
-                pltpu.VMEM((2, 2, R, LANES), bf16),
-                pltpu.VMEM((2, R, LANES), bf16),
-                pltpu.VMEM((2, R, LANES), bf16),
+                pltpu.VMEM((R + plan.half, LANES), bf16),
+                pltpu.VMEM((R + plan.half, LANES), bf16),
+                pltpu.VMEM((R + plan.half, LANES), bf16),
                 pltpu.VMEM((2, R, LANES), bf16),
                 pltpu.VMEM((HEAD_COUNT, rows, R), bf16),
-                dma((6,)),
-                dma((3, N)),
-                dma((3, N)),
-                dma,
-                dma,
-                dma((G // 2, B, N)),
-                dma((G // 2, B, N)),
-                dma((B, N)),
-                dma((B, N)),
+                dma((4,)),
+                dma((5,)),
+                dma((3, N - 1)),
+                dma((2,)),
+                dma((2,)),
                 dma((G // 2, B)),
                 dma((G // 2, B)),
-                dma((2,)),
-                dma((2,)),
+                dma((2, B - 1)),
+                dma((2, B - 1)),
+                dma((G // 2,)),
+                dma((G // 2,)),
+                dma((2, 2)),
             ],
             compiler_params=pltpu.CompilerParams(
                 collective_id=0, has_side_effects=True, vmem_limit_bytes=60 * 1024 * 1024

time: 25.3 us -> 22.5 us (0.89)
  Pallas kernels: 23.5 us -> 20.8 us
    pallas_call x1, Pallas kernels: 23.5 us -> 20.8 us  [per_device(): pl.pallas_call(functools.partial(kernel, plan), out_shape=jax.ShapeDtypeS...]
where the time goes in v2:
time: 22.5 us; the launch traced here: 22.4 us
  Pallas kernels  20.8 us (92%)
  local copies, waits for them, and re-layouts  1.62 us (7%)
    pallas_call x1, Pallas kernels, per_device(): pl.pallas_call(functools.partial(kernel, plan), out_shape=jax.ShapeDtypeS...  20.8 us
    unnamed x1, local copies, waits for them, and re-layouts  1.62 us

profile of v2, /device:TPU:0, one launch (start us, length us, event | category | flops | bytes accessed | tf_op | source)
XLA Modules:
  0.0 22.4 jit_solution(15051615080609585558)
XLA Ops:
  0.0 20.8 %shard_map.64 = bf16[128,768]{1,0:T(8,128)(2,1)} custom-call(bf16[128,384]{1,0:T(8,128)(2,1)} %q_hbm.1, bf16[128,384]{1,0:T(8,128)(2,1)} %k_hbm.1, bf16[128,384]{1,0:T(8,128)(2,1)} %v_hbm.1, s32[1,128]{1,0:T(1,128)} %bitcast.1, s32[2,6]{1,0:T(2,128)} %offs_hbm.1, bf16[384,768]{1,0:T(8,128)(2,1)} %w_hbm.1), custom_call_target="tpu_custom_call" | custom-call | tf_op jit(solution)/shard_map/pallas_call | solution.py:461
  20.8 1.6 %copy.8 = bf16[128,768]{1,0:T(8,128)(2,1)} copy(bf16[128,768]{1,0:T(8,128)(2,1)} %shard_map.64) | data formatting | bytes 393216

commit v3 on v2

--- a/solution.py
+++ b/solution.py
@@ -66,10 +66,16 @@
     return s
 
 
+def unfold(plan, x):
+    x = x.astype(jnp.float32)
+    low = pltpu.roll(x, HD, 1)[:plan.total - plan.half]
+    return jnp.concatenate([x, low], axis=0).astype(jnp.bfloat16)
+
+
 def kernel(
-    plan, q_hbm, k_hbm, v_hbm, valid_hbm, offs_hbm, w_hbm, o_ref,
-    qkv_ref, valid_ref, offs_ref, w_ref,
-    buf_a, buf_b, buf_c, snd_a, snd_b, snd_c, snd_q, own_q, got_q, ret_s, ret_r, own_o, back_hot,
+    plan, q_hbm, k_hbm, v_hbm, valid_hbm, offs_hbm, own_o, ret_r, back_hot,
+    qkv_ref, valid_ref, offs_ref,
+    buf_a, buf_b, buf_c, snd_a, snd_b, snd_c, snd_q, own_q, got_q, ret_s,
     load, zsend, zrecv, crecv, qsem, asend, arecv, bsend, brecv, fsend, frecv, rsem,
 ):
     G, B, N = plan.grp, plan.blk, plan.n
@@ -101,8 +107,7 @@
     load_offs = pltpu.make_async_copy(offs_hbm, offs_ref, load.at[0])
     load_valid = pltpu.make_async_copy(valid_hbm, valid_ref, load.at[1])
     load_qkv = [pltpu.make_async_copy(src, qkv_ref.at[n], load.at[2]) for n, src in enumerate((q_hbm, k_hbm, v_hbm))]
-    load_w = pltpu.make_async_copy(w_hbm, w_ref, load.at[3])
-    for copy in (load_offs, load_valid, *load_qkv, load_w):
+    for copy in (load_offs, load_valid, *load_qkv):
         copy.start()
     load_offs.wait()
     load_valid.wait()
@@ -133,10 +138,6 @@
         if R < 2 * H:
             low = jnp.concatenate([low, jnp.zeros((2 * H - R, LANES), low.dtype)], axis=0)
         return jnp.where(keep, x[:H], pltpu.roll(low, HD, 1))
-
-    def unfold(x):
-        x = x.astype(jnp.float32)
-        return jnp.concatenate([x, pltpu.roll(x, HD, 1)[:R - H]], axis=0).astype(jnp.bfloat16)
 
     packs = []
     for number, (a, b, c) in enumerate(SETS):
@@ -264,9 +265,6 @@
     spread_b(0, 0)
     send_line(2)
     spread_b(0, 1)
-    qcopy().start()
-    send_line(3)
-    send_line(4)
 
     token = lax.broadcasted_iota(jnp.int32, (plan.rows, R), 0)
     base, slot = plan.source(lax.broadcasted_iota(jnp.int32, (plan.rows, R), 1))
@@ -278,6 +276,9 @@
         zcopy(0, r).wait_recv()
         spread_a(r)
     fcopy(0, 0).start()
+    qcopy().start()
+    send_line(3)
+    send_line(4)
     for r in range(1, N):
         zcopy(1, r).wait_recv()
         spread_b(r, 0)
@@ -381,7 +382,7 @@
     qcopy().wait_recv()
     for x in range(K):
         arrived(buf_a.at[2 * x + 1], frecv.at[x])
-    got_single = unfold(got_q[R:R + H])
+    got_single = unfold(plan, got_q[R:R + H])
     outer, middle, dense = level_attend(2), level_attend(1), level_attend(0)
     third = outer((0, 1))
     value_half = left[:H] != even
@@ -422,11 +423,18 @@
             arrived(buf_b.at[0, :, heads[j]], bsend.at[j, y - 1])
     for x in range(K):
         arrived(buf_a.at[2 * x], fsend.at[x])
-    load_w.wait()
     for j in range(2):
         rcopy(j).wait_recv()
 
-    got = (ret_r[0:R], unfold(ret_r[R:R + H]))
+    for j in range(2):
+        rcopy(j).wait_send()
+
+
+def project(plan, own_o, ret_r, back_hot, w_ref, o_ref):
+    R, H = plan.total, plan.half
+    even = lax.axis_index("set") % 2 == 0
+    left = lax.broadcasted_iota(jnp.int32, (R, LANES), 1) < HD
+    got = (ret_r[0:R], unfold(plan, ret_r[R:R + H]))
     sets = [
         (jnp.where(even, own_o[j], got[j]), jnp.where(even, got[j], own_o[j])) for j in range(2)
     ]
@@ -442,9 +450,6 @@
     weights = jnp.concatenate(weights, axis=0)
     o_ref[...] = jnp.dot(attention, weights, preferred_element_type=jnp.float32).astype(o_ref.dtype)
 
-    for j in range(2):
-        rcopy(j).wait_send()
-
 
 def solution(mesh):
     G, B, N = mesh.shape["grp"], mesh.shape["blk"], mesh.shape["set"]
@@ -458,16 +463,19 @@
         ra, rb, rc = plan.sizes
         R = plan.total
         bf16 = jnp.bfloat16
-        return pl.pallas_call(
+        outputs = ((2, R, LANES), (R + plan.half, LANES), (HEAD_COUNT, rows, R))
+        attended = pl.pallas_call(
             functools.partial(kernel, plan),
-            out_shape=jax.ShapeDtypeStruct((rows, w_out.shape[1]), bf16),
-            in_specs=[anywhere] * 6,
-            out_specs=vmem,
+            out_shape=[pltpu.VMEM(shape, bf16) for shape in outputs],
+            in_specs=[anywhere] * 5,
+            out_specs=[vmem] * 3,
+            cost_estimate=pl.CostEstimate(
+                flops=4 * rows * rows * N * width * 4, bytes_accessed=4 * rows * width * 2, transcendentals=0
+            ),
             scratch_shapes=[
                 pltpu.VMEM((3, rows, width), bf16),
                 pltpu.VMEM((1, rows), jnp.int32),
                 pltpu.SMEM(offsets.shape, jnp.int32),
-                pltpu.VMEM(w_out.shape, bf16),
                 pltpu.VMEM((G, B, N, PARTS + 1, ra, LANES), bf16),
                 pltpu.VMEM((B, N, PARTS, rb, LANES), bf16),
                 pltpu.VMEM((N, PARTS, rc, LANES), bf16),
@@ -478,10 +486,7 @@
                 pltpu.VMEM((2, R, LANES), bf16),
                 pltpu.VMEM((R + plan.half, LANES), bf16),
                 pltpu.VMEM((R + plan.half, LANES), bf16),
-                pltpu.VMEM((R + plan.half, LANES), bf16),
-                pltpu.VMEM((2, R, LANES), bf16),
-                pltpu.VMEM((HEAD_COUNT, rows, R), bf16),
-                dma((4,)),
+                dma((3,)),
                 dma((5,)),
                 dma((3, N - 1)),
                 dma((2,)),
@@ -497,7 +502,14 @@
             compiler_params=pltpu.CompilerParams(
                 collective_id=0, has_side_effects=True, vmem_limit_bytes=60 * 1024 * 1024
             ),
-        )(queries, keys, values, valid.reshape(1, rows), offsets, w_out)
+        )(queries, keys, values, valid.reshape(1, rows), offsets)
+        return pl.pallas_call(
+            functools.partial(project, plan),
+            out_shape=jax.ShapeDtypeStruct((rows, w_out.shape[1]), bf16),
+            in_specs=[vmem] * 4,
+            out_specs=vmem,
+            compiler_params=pltpu.CompilerParams(vmem_limit_bytes=8 * 1024 * 1024),
+        )(*attended, w_out)
 
     rows_spec = P(("grp", "blk", "set"), None)
     return jax.shard_map(

time: 22.5 us -> 20.9 us (0.929)
  local copies, waits for them, and re-layouts: 1.62 us -> 0.01 us
    unnamed x1 -> x2, local copies, waits for them, and re-layouts: 1.62 us -> 0.01 us
    pallas_call x1 -> x2, Pallas kernels: 20.8 us -> 20.7 us  [the longest x1 19.6 us: per_device(): pl.pallas_call(functools.partial(kernel, plan), out_shape=[pltpu.VMEM(sha...]
where the time goes in v3:
time: 20.9 us; the launch traced here: 20.7 us
  Pallas kernels  20.7 us (99%)
    pallas_call x1, Pallas kernels, per_device(): pl.pallas_call(functools.partial(kernel, plan), out_shape=[pltpu.VMEM(sha...  19.6 us
    pallas_call x1, Pallas kernels, per_device(): pl.pallas_call(functools.partial(project, plan), out_shape=jax.ShapeDtype...  1.11 us

profile of v3, /device:TPU:0, one launch (start us, length us, event | category | flops | bytes accessed | tf_op | source)
XLA Modules:
  0.0 20.7 jit_solution(17065218018628921965)
XLA Ops:
  0.0 0.0 copy-start
  0.0 19.6 %shard_map.64 = (bf16[2,128,128]{2,1,0:T(8,128)(2,1)S(1)}, bf16[192,128]{1,0:T(8,128)(2,1)S(1)}, bf16[6,128,128]{2,1,0:T(8,128)(2,1)S(1)}) custom-call(bf16[128,384]{1,0:T(8,128)(2,1)} %q_hbm.1, bf16[128,384]{1,0:T(8,128)(2,1)} %k_hbm.1, bf16[128,384]{1,0:T(8,128)(2,1)} %v_hbm.1, s32[1,128]{1,0:T(1,128)} %bitcast.1, s32[2,6]{1,0:T(2,128)} %offs_hbm.1), custom_call_target="tpu_custom_call" | custom-call | flops 402653184 | bytes 393216 | tf_op jit(solution)/shard_map/pallas_call | solution.py:467
  19.6 0.0 copy-done
  19.6 1.1 %shard_map.65 = bf16[128,768]{1,0:T(8,128)(2,1)} custom-call(bf16[2,128,128]{2,1,0:T(8,128)(2,1)S(1)} %get-tuple-element.8.own_o, bf16[192,128]{1,0:T(8,128)(2,1)S(1)} %get-tuple-element.9.ret_r, bf16[6,128,128]{2,1,0:T(8,128)(2,1)S(1)} %get-tuple-element.10.back_hot, bf16[384,768]{1,0:T(8,128)(2,1)S(1)} %copy-done), custom_call_target="tpu_custom_call" | custom-call | tf_op jit(solution)/shard_map/pallas_call | solution.py:506
Async XLA Ops:
  0.0 19.6 %copy-start = (bf16[384,768]{1,0:T(8,128)(2,1)S(1)}, bf16[384,768]{1,0:T(8,128)(2,1)}, u32[]{:S(2)}) copy-start(bf16[384,768]{1,0:T(8,128)(2,1)} %w_ref.1) | copy-start | bytes 1769476

commit v4 on v3

--- a/solution.py
+++ b/solution.py
@@ -76,7 +76,7 @@
     plan, q_hbm, k_hbm, v_hbm, valid_hbm, offs_hbm, own_o, ret_r, back_hot,
     qkv_ref, valid_ref, offs_ref,
     buf_a, buf_b, buf_c, snd_a, snd_b, snd_c, snd_q, own_q, got_q, ret_s,
-    load, zsend, zrecv, crecv, qsem, asend, arecv, bsend, brecv, fsend, frecv, rsem,
+    load, zsend, zrecv, crecv, qsem, asend, afirst, arecv, bsend, brecv, fsend, frecv, rsem,
 ):
     G, B, N = plan.grp, plan.blk, plan.n
     R = plan.total
@@ -91,7 +91,9 @@
         return (lax.rem(gi + 2 * sx, G), lax.rem(bi + sy, B), si)
 
 
-    across = [(sx, sy) for sx in range(K) for sy in range(B) if sx or sy]
+    across = [(x, y) for x in range(K) for y in range(B) if x or y]
+    near = [(x, y) for x, y in across if not (x and y)]
+    diagonal = [(x, y) for x, y in across if x and y]
 
     barrier = pltpu.get_barrier_semaphore()
 
@@ -100,8 +102,8 @@
 
     for r in range(N - 1, 0, -1):
         greet((gi, bi, flip(si, r)))
-    for sx, sy in across:
-        greet(peer(sx, sy))
+    for x, y in near:
+        greet(peer(x, y))
     greet((partner, bi, si))
 
     load_offs = pltpu.make_async_copy(offs_hbm, offs_ref, load.at[0])
@@ -177,7 +179,7 @@
     snd_q[0:R] = other[3]
     snd_q[R:R + H] = other[6]
 
-    pl.semaphore_wait(barrier, (N - 1) + len(across) + 1)
+    pl.semaphore_wait(barrier, (N - 1) + len(near) + 1)
 
     heads = (slice(0, 2), slice(2, 3))
     line_sem = (lambda r: zrecv.at[0, r - 1], lambda r: zrecv.at[1, r - 1], lambda r: zrecv.at[2, r - 1])
@@ -217,7 +219,8 @@
     def acopy(x, y, r):
         return pltpu.make_async_remote_copy(
             src_ref=buf_a.at[0, 0, r], dst_ref=buf_a.at[2 * x, y, r],
-            send_sem=asend.at[x, y], recv_sem=arecv.at[x, y],
+            send_sem=asend.at[x, y],
+            recv_sem=afirst.at[y - 1] if x == 0 and r == 0 else arecv.at[x, y],
             device_id=peer((K - x) % K, (B - y) % B), device_id_type=MESH,
         )
 
@@ -245,8 +248,8 @@
     def arrived(ref, sem):
         pltpu.make_async_copy(ref, ref, sem).wait()
 
-    def spread_a(r):
-        for x, y in across:
+    def spread_a(r, where):
+        for x, y in where:
             acopy(x, y, r).start()
 
     def spread_b(r, j):
@@ -260,7 +263,7 @@
             zcopy(part, r).start()
 
     send_line(0)
-    spread_a(0)
+    spread_a(0, near)
     send_line(1)
     spread_b(0, 0)
     send_line(2)
@@ -272,9 +275,12 @@
         hit = token == base + ((slot + offs_ref[1, h]) & (plan.period - 1))
         back_hot[h] = jnp.where(hit, jnp.float32(1), jnp.float32(0)).astype(jnp.bfloat16)
 
+    for y in range(1, B):
+        acopy(0, y, 0).wait_recv()
+    spread_a(0, diagonal)
     for r in range(1, N):
         zcopy(0, r).wait_recv()
-        spread_a(r)
+        spread_a(r, across)
     fcopy(0, 0).start()
     qcopy().start()
     send_line(3)
@@ -286,7 +292,7 @@
         zcopy(2, r).wait_recv()
         spread_b(r, 1)
     for x, y in across:
-        arrived(buf_a.at[2 * x, y], arecv.at[x, y])
+        arrived(buf_a.at[2 * x, y] if x else buf_a.at[0, y, 1:N], arecv.at[x, y])
         fcopy(x, y).start()
 
     head_pick = lax.broadcasted_iota(jnp.int32, (FLAG_STRIDE, LANES), 1) & (FLAG_STRIDE - 1)
@@ -492,6 +498,7 @@
                 dma((2,)),
                 dma((2,)),
                 dma((G // 2, B)),
+                dma((B - 1,)),
                 dma((G // 2, B)),
                 dma((2, B - 1)),
                 dma((2, B - 1)),

time: 20.9 us -> 20.9 us (level)
  no operation moved by 1% of the time
where the time goes in v4:
time: 20.9 us; the launch traced here: 20.7 us
  Pallas kernels  20.7 us (99%)
    pallas_call x1, Pallas kernels, per_device(): pl.pallas_call(functools.partial(kernel, plan), out_shape=[pltpu.VMEM(sha...  19.6 us
    pallas_call x1, Pallas kernels, per_device(): pl.pallas_call(functools.partial(project, plan), out_shape=jax.ShapeDtype...  1.11 us

profile of v4, /device:TPU:0, one launch (start us, length us, event | category | flops | bytes accessed | tf_op | source)
XLA Modules:
  0.0 20.7 jit_solution(3761697788953753807)
XLA Ops:
  0.0 0.0 copy-start
  0.0 19.6 %shard_map.64 = (bf16[2,128,128]{2,1,0:T(8,128)(2,1)S(1)}, bf16[192,128]{1,0:T(8,128)(2,1)S(1)}, bf16[6,128,128]{2,1,0:T(8,128)(2,1)S(1)}) custom-call(bf16[128,384]{1,0:T(8,128)(2,1)} %q_hbm.1, bf16[128,384]{1,0:T(8,128)(2,1)} %k_hbm.1, bf16[128,384]{1,0:T(8,128)(2,1)} %v_hbm.1, s32[1,128]{1,0:T(1,128)} %bitcast.1, s32[2,6]{1,0:T(2,128)} %offs_hbm.1), custom_call_target="tpu_custom_call" | custom-call | flops 402653184 | bytes 393216 | tf_op jit(solution)/shard_map/pallas_call | solution.py:473
  19.6 0.0 copy-done
  19.6 1.1 %shard_map.65 = bf16[128,768]{1,0:T(8,128)(2,1)} custom-call(bf16[2,128,128]{2,1,0:T(8,128)(2,1)S(1)} %get-tuple-element.8.own_o, bf16[192,128]{1,0:T(8,128)(2,1)S(1)} %get-tuple-element.9.ret_r, bf16[6,128,128]{2,1,0:T(8,128)(2,1)S(1)} %get-tuple-element.10.back_hot, bf16[384,768]{1,0:T(8,128)(2,1)S(1)} %copy-done), custom_call_target="tpu_custom_call" | custom-call | tf_op jit(solution)/shard_map/pallas_call | solution.py:513
Async XLA Ops:
  0.0 19.6 %copy-start = (bf16[384,768]{1,0:T(8,128)(2,1)S(1)}, bf16[384,768]{1,0:T(8,128)(2,1)}, u32[]{:S(2)}) copy-start(bf16[384,768]{1,0:T(8,128)(2,1)} %w_ref.1) | copy-start | bytes 1769476

commit v5 on v4

--- a/solution.py
+++ b/solution.py
@@ -331,11 +331,24 @@
             head_pick, tall, (((1,), (1,)), ((), ())), preferred_element_type=jnp.float32
         )
         keys = per_unit * tiles
-        row = lax.broadcasted_iota(jnp.int32, (2 * M, keys), 0)
-        who = jnp.where(row < M, 0, 1)
-        t = row - who * M
-        spot = (t // UNIT) * per_unit + (t % UNIT) + who * UNIT
-        own = lax.broadcasted_iota(jnp.int32, (2 * M, keys), 1) == spot
+        diagonal_tile = lax.broadcasted_iota(jnp.int32, (UNIT, LANES), 1) - lax.broadcasted_iota(
+            jnp.int32, (UNIT, LANES), 0
+        )
+
+        def allow(s, bias):
+            masked = s + bias
+            rows = []
+            for who in range(2):
+                for u in range(tiles):
+                    at = slice((who * tiles + u) * UNIT, (who * tiles + u + 1) * UNIT)
+                    spot = u * per_unit + who * UNIT
+                    tile = slice(spot // LANES * LANES, spot // LANES * LANES + LANES)
+                    fixed = jnp.where(diagonal_tile == spot % LANES, s[at, tile], masked[at, tile])
+                    pieces = [masked[at, :tile.start], fixed, masked[at, tile.stop:]]
+                    rows.append(jnp.concatenate([p for p in pieces if p.shape[1]], axis=1))
+            return jnp.concatenate(rows, axis=0)
+
+        bias = jnp.where(ok > 0.5, 0.0, NEG)
         half_lane = lax.broadcasted_iota(jnp.int32, (2 * M, LANES), 1) < HD
         value_lane = half_lane != even
         contract = (((1,), (1,)), ((), ()))
@@ -344,41 +357,45 @@
         def query(j):
             return jnp.concatenate([own_q[j, 0:M], got_q[0:M] if j == 0 else got_single[0:M]], axis=0)
 
-        def run(parts):
-            scores = []
-            if 0 in parts:
-                q = query(0)
-                both = jnp.concatenate([jnp.where(half_lane, q, zero), jnp.where(half_lane, zero, q)], axis=0)
-                both = lax.dot_general(both, gather(level, 0), contract, preferred_element_type=jnp.float32)
-                scores += [both[:2 * M], both[2 * M:]]
-            if 1 in parts:
-                single = gather(level, 2)
-                q = jnp.where(value_lane, zero, query(1))
-                scores.append(lax.dot_general(q, single, contract, preferred_element_type=jnp.float32))
-            first = 0 if 0 in parts else 2
-            scores = [jnp.where(own | (ok[first + n:first + n + 1, :] > 0.5), s, NEG) for n, s in enumerate(scores)]
-            tops = [jnp.max(s, axis=1, keepdims=True) for s in scores]
-            weights = [jnp.exp(s - top) for s, top in zip(scores, tops)]
-            probs = [w.astype(jnp.bfloat16) for w in weights]
-            results = []
-            if 0 in parts:
-                pair = jnp.dot(jnp.concatenate(probs[:2], axis=0), gather(level, 1), preferred_element_type=jnp.float32)
-            if 1 in parts:
-                alone = jnp.dot(probs[-1], single, preferred_element_type=jnp.float32)
-            totals = [jnp.sum(w, axis=1, keepdims=True) for w in weights]
-            lses = [top + jnp.log(total) for top, total in zip(tops, totals)]
-            if 0 in parts:
-                results.append(
-                    (
-                        jnp.where(half_lane, pair[:2 * M] / totals[0], pair[2 * M:] / totals[1]),
-                        jnp.where(half_lane, lses[0], lses[1]),
-                    )
-                )
-            if 1 in parts:
-                results.append((alone / totals[-1], jnp.broadcast_to(lses[-1], (2 * M, LANES))))
-            return results
-
-        return run
+        def scores(part):
+            q = query(part)
+            keys = gather(level, 2 * part)
+            if part == 0:
+                q = jnp.concatenate([jnp.where(half_lane, q, zero), jnp.where(half_lane, zero, q)], axis=0)
+            else:
+                q = jnp.where(value_lane, zero, q)
+            s = lax.dot_general(q, keys, contract, preferred_element_type=jnp.float32)
+            return [s[:2 * M], s[2 * M:]] if part == 0 else [s]
+
+        def masked(s, part):
+            return [allow(x, bias[2 * part + n:2 * part + n + 1, :]) for n, x in enumerate(s)]
+
+        def mix(probs, part):
+            values = gather(level, 1 + part)
+            return jnp.dot(jnp.concatenate(probs, axis=0), values, preferred_element_type=jnp.float32)
+
+        def finish(mixed, totals, lses, part):
+            if part == 1:
+                return mixed / totals[0], jnp.broadcast_to(lses[0], (2 * M, LANES))
+            return (
+                jnp.where(half_lane, mixed[:2 * M] / totals[0], mixed[2 * M:] / totals[1]),
+                jnp.where(half_lane, lses[0], lses[1]),
+            )
+
+        return scores, masked, mix, finish
+
+    def attend(jobs):
+        scores = [level[0](part) for level, part in jobs]
+        scores = [level[1](s, part) for s, (level, part) in zip(scores, jobs)]
+        tops = [[jnp.max(x, axis=1, keepdims=True) for x in s] for s in scores]
+        weights = [[jnp.exp(x - t) for x, t in zip(s, top)] for s, top in zip(scores, tops)]
+        probs = [[x.astype(jnp.bfloat16) for x in w] for w in weights]
+        mixed = [level[2](p, part) for p, (level, part) in zip(probs, jobs)]
+        totals = [[jnp.sum(x, axis=1, keepdims=True) for x in w] for w in weights]
+        lses = [[t + jnp.log(x) for t, x in zip(top, total)] for top, total in zip(tops, totals)]
+        return [
+            level[3](m, total, lse, part) for m, total, lse, (level, part) in zip(mixed, totals, lses, jobs)
+        ]
 
     def combine(levels):
         top = functools.reduce(jnp.maximum, [lse for _, lse in levels])
@@ -390,14 +407,16 @@
         arrived(buf_a.at[2 * x + 1], frecv.at[x])
     got_single = unfold(plan, got_q[R:R + H])
     outer, middle, dense = level_attend(2), level_attend(1), level_attend(0)
-    third = outer((0, 1))
     value_half = left[:H] != even
     for j in range(2):
         for y in range(1, B):
             arrived(buf_b.at[y, :, heads[j]], brecv.at[j, y - 1])
-        second = middle((j,))[0]
         arrived(buf_c.at[1:N, heads[j]], crecv.at[j])
-        first = dense((j,))[0]
+        jobs = [(middle, j), (dense, j)]
+        if j == 0:
+            second, first, *third = attend(jobs + [(outer, 0), (outer, 1)])
+        else:
+            second, first = attend(jobs)
         for who in (1, 0):
             (o1, l1), (o2, l2), (o3, l3) = [
                 tuple(x[who * m:(who + 1) * m] for x in level)

time: 20.9 us -> 20.2 us (0.967)
  Pallas kernels: 20.7 us -> 20 us
    pallas_call x1, Pallas kernels: 19.6 us -> 18.9 us  [per_device(): pl.pallas_call(functools.partial(kernel, plan), out_shape=[pltpu.VMEM(sha...]
where the time goes in v5:
time: 20.2 us; the launch traced here: 20 us
  Pallas kernels  20 us (99%)
    pallas_call x1, Pallas kernels, per_device(): pl.pallas_call(functools.partial(kernel, plan), out_shape=[pltpu.VMEM(sha...  18.9 us
    pallas_call x1, Pallas kernels, per_device(): pl.pallas_call(functools.partial(project, plan), out_shape=jax.ShapeDtype...  1.11 us

profile of v5, /device:TPU:0, one launch (start us, length us, event | category | flops | bytes accessed | tf_op | source)
XLA Modules:
  0.0 20.0 jit_solution(18080758692826499932)
XLA Ops:
  0.0 0.0 copy-start
  0.0 18.9 %shard_map.64 = (bf16[2,128,128]{2,1,0:T(8,128)(2,1)S(1)}, bf16[192,128]{1,0:T(8,128)(2,1)S(1)}, bf16[6,128,128]{2,1,0:T(8,128)(2,1)S(1)}) custom-call(bf16[128,384]{1,0:T(8,128)(2,1)} %q_hbm.1, bf16[128,384]{1,0:T(8,128)(2,1)} %k_hbm.1, bf16[128,384]{1,0:T(8,128)(2,1)} %v_hbm.1, s32[1,128]{1,0:T(1,128)} %bitcast.1, s32[2,6]{1,0:T(2,128)} %offs_hbm.1), custom_call_target="tpu_custom_call" | custom-call | flops 402653184 | bytes 393216 | tf_op jit(solution)/shard_map/pallas_call | solution.py:492
  18.9 0.0 copy-done
  18.9 1.1 %shard_map.65 = bf16[128,768]{1,0:T(8,128)(2,1)} custom-call(bf16[2,128,128]{2,1,0:T(8,128)(2,1)S(1)} %get-tuple-element.8.own_o, bf16[192,128]{1,0:T(8,128)(2,1)S(1)} %get-tuple-element.9.ret_r, bf16[6,128,128]{2,1,0:T(8,128)(2,1)S(1)} %get-tuple-element.10.back_hot, bf16[384,768]{1,0:T(8,128)(2,1)S(1)} %copy-done), custom_call_target="tpu_custom_call" | custom-call | tf_op jit(solution)/shard_map/pallas_call | solution.py:532
Async XLA Ops:
  0.0 18.9 %copy-start = (bf16[384,768]{1,0:T(8,128)(2,1)S(1)}, bf16[384,768]{1,0:T(8,128)(2,1)}, u32[]{:S(2)}) copy-start(bf16[384,768]{1,0:T(8,128)(2,1)} %w_ref.1) | copy-start | bytes 1769476

commit v6 on v5

--- a/solution.py
+++ b/solution.py
@@ -91,6 +91,12 @@
         return (lax.rem(gi + 2 * sx, G), lax.rem(bi + sy, B), si)
 
 
+    load_offs = pltpu.make_async_copy(offs_hbm, offs_ref, load.at[0])
+    load_valid = pltpu.make_async_copy(valid_hbm, valid_ref, load.at[1])
+    load_qkv = [pltpu.make_async_copy(src, qkv_ref.at[n], load.at[2]) for n, src in enumerate((q_hbm, k_hbm, v_hbm))]
+    for copy in (*load_qkv, load_offs, load_valid):
+        copy.start()
+
     across = [(x, y) for x in range(K) for y in range(B) if x or y]
     near = [(x, y) for x, y in across if not (x and y)]
     diagonal = [(x, y) for x, y in across if x and y]
@@ -106,11 +112,6 @@
         greet(peer(x, y))
     greet((partner, bi, si))
 
-    load_offs = pltpu.make_async_copy(offs_hbm, offs_ref, load.at[0])
-    load_valid = pltpu.make_async_copy(valid_hbm, valid_ref, load.at[1])
-    load_qkv = [pltpu.make_async_copy(src, qkv_ref.at[n], load.at[2]) for n, src in enumerate((q_hbm, k_hbm, v_hbm))]
-    for copy in (load_offs, load_valid, *load_qkv):
-        copy.start()
     load_offs.wait()
     load_valid.wait()
     pltpu.make_async_copy(qkv_ref, qkv_ref, load.at[2]).wait()
@@ -124,13 +125,17 @@
 
     moved = {}
     columns = {}
-    for h in range(HEAD_COUNT):
-        cols = slice((h // 2) * LANES, (h // 2 + 1) * LANES)
+    for c in range(CHUNKS):
+        cols = slice(c * LANES, (c + 1) * LANES)
         packed = jnp.concatenate([qkv_ref[n, :, cols] for n in range(3)], axis=1)
-        hit = token == base + ((slot + offs_ref[1, h]) & (plan.period - 1))
-        onehot = jnp.where(hit, jnp.float32(1), jnp.float32(0))
-        moved[h] = jnp.dot(onehot.astype(jnp.bfloat16), packed, preferred_element_type=jnp.float32)
-        columns[h] = jnp.sum(onehot * valid_row, axis=1, keepdims=True)
+        hits = []
+        for h in (2 * c, 2 * c + 1):
+            hit = token == base + ((slot + offs_ref[1, h]) & (plan.period - 1))
+            onehot = jnp.where(hit, jnp.float32(1), jnp.float32(0))
+            columns[h] = jnp.sum(onehot * valid_row, axis=1, keepdims=True)
+            hits.append(onehot.astype(jnp.bfloat16))
+        both = jnp.dot(jnp.concatenate(hits, axis=0), packed, preferred_element_type=jnp.float32)
+        moved[2 * c], moved[2 * c + 1] = both[:R], both[R:]
 
     def piece(h, which):
         return moved[h][:, which * LANES:(which + 1) * LANES]
@@ -335,72 +340,69 @@
             jnp.int32, (UNIT, LANES), 0
         )
 
-        def allow(s, bias):
+        def allow(s, bias, who):
             masked = s + bias
             rows = []
-            for who in range(2):
-                for u in range(tiles):
-                    at = slice((who * tiles + u) * UNIT, (who * tiles + u + 1) * UNIT)
-                    spot = u * per_unit + who * UNIT
-                    tile = slice(spot // LANES * LANES, spot // LANES * LANES + LANES)
-                    fixed = jnp.where(diagonal_tile == spot % LANES, s[at, tile], masked[at, tile])
-                    pieces = [masked[at, :tile.start], fixed, masked[at, tile.stop:]]
-                    rows.append(jnp.concatenate([p for p in pieces if p.shape[1]], axis=1))
+            for u in range(tiles):
+                at = slice(u * UNIT, (u + 1) * UNIT)
+                spot = u * per_unit + who * UNIT
+                tile = slice(spot // LANES * LANES, spot // LANES * LANES + LANES)
+                fixed = jnp.where(diagonal_tile == spot % LANES, s[at, tile], masked[at, tile])
+                pieces = [masked[at, :tile.start], fixed, masked[at, tile.stop:]]
+                rows.append(jnp.concatenate([p for p in pieces if p.shape[1]], axis=1))
             return jnp.concatenate(rows, axis=0)
 
         bias = jnp.where(ok > 0.5, 0.0, NEG)
-        half_lane = lax.broadcasted_iota(jnp.int32, (2 * M, LANES), 1) < HD
+        half_lane = lax.broadcasted_iota(jnp.int32, (M, LANES), 1) < HD
         value_lane = half_lane != even
         contract = (((1,), (1,)), ((), ()))
-        zero = jnp.zeros((2 * M, LANES), jnp.bfloat16)
-
-        def query(j):
-            return jnp.concatenate([own_q[j, 0:M], got_q[0:M] if j == 0 else got_single[0:M]], axis=0)
-
-        def scores(part):
-            q = query(part)
+        zero = jnp.zeros((M, LANES), jnp.bfloat16)
+
+        def scores(part, who):
+            q = own_q[part, 0:M] if who == 0 else got_q[0:M] if part == 0 else got_single[0:M]
             keys = gather(level, 2 * part)
             if part == 0:
                 q = jnp.concatenate([jnp.where(half_lane, q, zero), jnp.where(half_lane, zero, q)], axis=0)
             else:
                 q = jnp.where(value_lane, zero, q)
             s = lax.dot_general(q, keys, contract, preferred_element_type=jnp.float32)
-            return [s[:2 * M], s[2 * M:]] if part == 0 else [s]
-
-        def masked(s, part):
-            return [allow(x, bias[2 * part + n:2 * part + n + 1, :]) for n, x in enumerate(s)]
+            return [s[:M], s[M:]] if part == 0 else [s]
+
+        def masked(s, part, who):
+            return [allow(x, bias[2 * part + n:2 * part + n + 1, :], who) for n, x in enumerate(s)]
 
         def mix(probs, part):
             values = gather(level, 1 + part)
             return jnp.dot(jnp.concatenate(probs, axis=0), values, preferred_element_type=jnp.float32)
 
-        def finish(mixed, totals, lses, part):
+        def finish(mixed, tops, totals, part):
             if part == 1:
-                return mixed / totals[0], jnp.broadcast_to(lses[0], (2 * M, LANES))
+                return (mixed, *(jnp.broadcast_to(x[0], (M, LANES)) for x in (tops, totals)))
             return (
-                jnp.where(half_lane, mixed[:2 * M] / totals[0], mixed[2 * M:] / totals[1]),
-                jnp.where(half_lane, lses[0], lses[1]),
+                jnp.where(half_lane, mixed[:M], mixed[M:]),
+                *(jnp.where(half_lane, x[0], x[1]) for x in (tops, totals)),
             )
 
         return scores, masked, mix, finish
 
-    def attend(jobs):
-        scores = [level[0](part) for level, part in jobs]
-        scores = [level[1](s, part) for s, (level, part) in zip(scores, jobs)]
+    def attend(jobs, who):
+        scores = [level[0](part, who) for level, part in jobs]
+        scores = [level[1](s, part, who) for s, (level, part) in zip(scores, jobs)]
         tops = [[jnp.max(x, axis=1, keepdims=True) for x in s] for s in scores]
         weights = [[jnp.exp(x - t) for x, t in zip(s, top)] for s, top in zip(scores, tops)]
         probs = [[x.astype(jnp.bfloat16) for x in w] for w in weights]
         mixed = [level[2](p, part) for p, (level, part) in zip(probs, jobs)]
         totals = [[jnp.sum(x, axis=1, keepdims=True) for x in w] for w in weights]
-        lses = [[t + jnp.log(x) for t, x in zip(top, total)] for top, total in zip(tops, totals)]
         return [
-            level[3](m, total, lse, part) for m, total, lse, (level, part) in zip(mixed, totals, lses, jobs)
+            level[3](m, top, total, part) for m, top, total, (level, part) in zip(mixed, tops, totals, jobs)
         ]
 
-    def combine(levels):
-        top = functools.reduce(jnp.maximum, [lse for _, lse in levels])
-        shares = [jnp.exp(lse - top) for _, lse in levels]
-        return sum(s * o for s, (o, _) in zip(shares, levels)) / sum(shares)
+    def combine(*levels):
+        highest = functools.reduce(jnp.maximum, [top for _, top, _ in levels])
+        shares = [jnp.exp(top - highest) for _, top, _ in levels]
+        return sum(s * m for s, (m, _, _) in zip(shares, levels)) / sum(
+            s * total for s, (_, _, total) in zip(shares, levels)
+        )
 
     qcopy().wait_recv()
     for x in range(K):
@@ -408,36 +410,37 @@
     got_single = unfold(plan, got_q[R:R + H])
     outer, middle, dense = level_attend(2), level_attend(1), level_attend(0)
     value_half = left[:H] != even
-    for j in range(2):
-        for y in range(1, B):
-            arrived(buf_b.at[y, :, heads[j]], brecv.at[j, y - 1])
-        arrived(buf_c.at[1:N, heads[j]], crecv.at[j])
+    for who, j in ((1, 0), (1, 1), (0, 0), (0, 1)):
+        if who == 1:
+            for y in range(1, B):
+                arrived(buf_b.at[y, :, heads[j]], brecv.at[j, y - 1])
+            arrived(buf_c.at[1:N, heads[j]], crecv.at[j])
         jobs = [(middle, j), (dense, j)]
         if j == 0:
-            second, first, *third = attend(jobs + [(outer, 0), (outer, 1)])
+            second, first, *third = attend(jobs + [(outer, 0), (outer, 1)], who)
         else:
-            second, first = attend(jobs)
-        for who in (1, 0):
-            (o1, l1), (o2, l2), (o3, l3) = [
-                tuple(x[who * m:(who + 1) * m] for x in level)
-                for level, m in ((first, R), (second, b_end), (third[j], a_end))
-            ]
-            mixed = jnp.concatenate(
-                [
-                    combine([(o1[:a_end], l1[:a_end]), (o2[:a_end], l2[:a_end]), (o3, l3)]),
-                    combine([(o1[a_end:b_end], l1[a_end:b_end]), (o2[a_end:], l2[a_end:])]),
-                    o1[b_end:],
-                ],
-                axis=0,
-            )
-            if who == 0:
-                own_o[j] = mixed.astype(jnp.bfloat16)
+            second, first = attend(jobs, who)
+
+        def rows(level, start, stop):
+            return tuple(x[start:stop] for x in level)
+
+        alone = rows(first, b_end, R)
+        mixed = jnp.concatenate(
+            [
+                combine(rows(first, 0, a_end), rows(second, 0, a_end), third[j]),
+                combine(rows(first, a_end, b_end), rows(second, a_end, b_end)),
+                alone[0] / alone[2],
+            ],
+            axis=0,
+        )
+        if who == 0:
+            own_o[j] = mixed.astype(jnp.bfloat16)
+        else:
+            if j == 0:
+                ret_s[0:R] = mixed.astype(jnp.bfloat16)
             else:
-                if j == 0:
-                    ret_s[0:R] = mixed.astype(jnp.bfloat16)
-                else:
-                    ret_s[R:R + H] = fold(mixed, value_half).astype(jnp.bfloat16)
-                rcopy(j).start()
+                ret_s[R:R + H] = fold(mixed, value_half).astype(jnp.bfloat16)
+            rcopy(j).start()
     for part in range(5):
         line_sent(part)
     qcopy().wait_send()

time: 20.2 us -> 19.9 us (0.985)
  Pallas kernels: 20 us -> 19.7 us
    pallas_call x1, Pallas kernels: 18.9 us -> 18.6 us  [per_device(): pl.pallas_call(functools.partial(kernel, plan), out_shape=[pltpu.VMEM(sha...]
where the time goes in v6:
time: 19.9 us; the launch traced here: 19.7 us
  Pallas kernels  19.7 us (99%)
    pallas_call x1, Pallas kernels, per_device(): pl.pallas_call(functools.partial(kernel, plan), out_shape=[pltpu.VMEM(sha...  18.6 us
    pallas_call x1, Pallas kernels, per_device(): pl.pallas_call(functools.partial(project, plan), out_shape=jax.ShapeDtype...  1.11 us

profile of v6, /device:TPU:0, one launch (start us, length us, event | category | flops | bytes accessed | tf_op | source)
XLA Modules:
  0.0 19.7 jit_solution(6110060000935244352)
XLA Ops:
  0.0 0.0 copy-start
  0.0 18.6 %shard_map.64 = (bf16[2,128,128]{2,1,0:T(8,128)(2,1)S(1)}, bf16[192,128]{1,0:T(8,128)(2,1)S(1)}, bf16[6,128,128]{2,1,0:T(8,128)(2,1)S(1)}) custom-call(bf16[128,384]{1,0:T(8,128)(2,1)} %q_hbm.1, bf16[128,384]{1,0:T(8,128)(2,1)} %k_hbm.1, bf16[128,384]{1,0:T(8,128)(2,1)} %v_hbm.1, s32[1,128]{1,0:T(1,128)} %bitcast.1, s32[2,6]{1,0:T(2,128)} %offs_hbm.1), custom_call_target="tpu_custom_call" | custom-call | flops 402653184 | bytes 393216 | tf_op jit(solution)/shard_map/pallas_call | solution.py:495
  18.6 0.0 copy-done
  18.6 1.1 %shard_map.65 = bf16[128,768]{1,0:T(8,128)(2,1)} custom-call(bf16[2,128,128]{2,1,0:T(8,128)(2,1)S(1)} %get-tuple-element.8.own_o, bf16[192,128]{1,0:T(8,128)(2,1)S(1)} %get-tuple-element.9.ret_r, bf16[6,128,128]{2,1,0:T(8,128)(2,1)S(1)} %get-tuple-element.10.back_hot, bf16[384,768]{1,0:T(8,128)(2,1)S(1)} %copy-done), custom_call_target="tpu_custom_call" | custom-call | tf_op jit(solution)/shard_map/pallas_call | solution.py:535
Async XLA Ops:
  0.0 18.6 %copy-start = (bf16[384,768]{1,0:T(8,128)(2,1)S(1)}, bf16[384,768]{1,0:T(8,128)(2,1)}, u32[]{:S(2)}) copy-start(bf16[384,768]{1,0:T(8,128)(2,1)} %w_ref.1) | copy-start | bytes 1769476

commit v7 on v6

--- a/solution.py
+++ b/solution.py
@@ -405,10 +405,11 @@
         )
 
     qcopy().wait_recv()
+    got_single = unfold(plan, got_q[R:R + H])
+    middle, dense = level_attend(1), level_attend(0)
     for x in range(K):
         arrived(buf_a.at[2 * x + 1], frecv.at[x])
-    got_single = unfold(plan, got_q[R:R + H])
-    outer, middle, dense = level_attend(2), level_attend(1), level_attend(0)
+    outer = level_attend(2)
     value_half = left[:H] != even
     for who, j in ((1, 0), (1, 1), (0, 0), (0, 1)):
         if who == 1:

time: 19.9 us -> 19.9 us (level)
  no operation moved by 1% of the time
where the time goes in v7:
time: 19.9 us; the launch traced here: 19.7 us
  Pallas kernels  19.7 us (99%)
    pallas_call x1, Pallas kernels, per_device(): pl.pallas_call(functools.partial(kernel, plan), out_shape=[pltpu.VMEM(sha...  18.6 us
    pallas_call x1, Pallas kernels, per_device(): pl.pallas_call(functools.partial(project, plan), out_shape=jax.ShapeDtype...  1.11 us

profile of v7, /device:TPU:0, one launch (start us, length us, event | category | flops | bytes accessed | tf_op | source)
XLA Modules:
  0.0 19.7 jit_solution(3784459315518112300)
XLA Ops:
  0.0 0.0 copy-start
  0.0 18.6 %shard_map.64 = (bf16[2,128,128]{2,1,0:T(8,128)(2,1)S(1)}, bf16[192,128]{1,0:T(8,128)(2,1)S(1)}, bf16[6,128,128]{2,1,0:T(8,128)(2,1)S(1)}) custom-call(bf16[128,384]{1,0:T(8,128)(2,1)} %q_hbm.1, bf16[128,384]{1,0:T(8,128)(2,1)} %k_hbm.1, bf16[128,384]{1,0:T(8,128)(2,1)} %v_hbm.1, s32[1,128]{1,0:T(1,128)} %bitcast.1, s32[2,6]{1,0:T(2,128)} %offs_hbm.1), custom_call_target="tpu_custom_call" | custom-call | flops 402653184 | bytes 393216 | tf_op jit(solution)/shard_map/pallas_call | solution.py:496
  18.6 0.0 copy-done
  18.6 1.1 %shard_map.65 = bf16[128,768]{1,0:T(8,128)(2,1)} custom-call(bf16[2,128,128]{2,1,0:T(8,128)(2,1)S(1)} %get-tuple-element.8.own_o, bf16[192,128]{1,0:T(8,128)(2,1)S(1)} %get-tuple-element.9.ret_r, bf16[6,128,128]{2,1,0:T(8,128)(2,1)S(1)} %get-tuple-element.10.back_hot, bf16[384,768]{1,0:T(8,128)(2,1)S(1)} %copy-done), custom_call_target="tpu_custom_call" | custom-call | tf_op jit(solution)/shard_map/pallas_call | solution.py:536
Async XLA Ops:
  0.0 18.6 %copy-start = (bf16[384,768]{1,0:T(8,128)(2,1)S(1)}, bf16[384,768]{1,0:T(8,128)(2,1)}, u32[]{:S(2)}) copy-start(bf16[384,768]{1,0:T(8,128)(2,1)} %w_ref.1) | copy-start | bytes 1769476
